TPU v7x, 32 devices: a 4x4x1 block of a 4x4x8 slice. The times are simulated.
32 devices in a mesh: dp: 1 (over z), ep: 32 (over y, x, core).
Axes of the slice: x: 4, y: 4, z: 1, core: 2. Of those that a mesh axis runs over, the one named last changes fastest.
The devices are a block of a 4x4x8 slice.
Arguments:
- x: bfloat16 [24576, 2048], P(('dp', 'ep'))
- route_idx: int32 [24576, 8], P(('dp', 'ep'))
- gates: bfloat16 [24576, 8], P(('dp', 'ep'))
- w1: bfloat16 [96, 2048, 1024], P('ep')
- w3: bfloat16 [96, 2048, 1024], P('ep')
- w2: bfloat16 [96, 1024, 2048], P('ep')
Outputs:
- output: bfloat16 [24576, 2048], P(('dp', 'ep'))
All inputs are finite; a program needn't handle non-finite values.
Results may differ from a plain program's by a relative error of at most 0.00142.
Values are sent between devices in bfloat16 or wider.
A program may use at most 768 MiB of HBM per device.

v0:
```python
import jax
import jax.numpy as jnp
from jax import lax
from jax.sharding import PartitionSpec as P

BLK = 128


def holder_list(p):
    return [0, (p // 2 + 1) % p, (p // 4 + 2) % p, (3 * p // 4 + 3) % p]


def counting(ids, ng):
    n = ids.shape[0]
    nb = -(-n // BLK)
    idp = jnp.pad(ids, (0, nb * BLK - n), constant_values=ng).reshape(nb, BLK, 1)
    oh = (idp == jnp.arange(ng, dtype=ids.dtype)).astype(jnp.bfloat16)
    tri = (jnp.arange(BLK)[:, None] > jnp.arange(BLK)[None, :]).astype(jnp.bfloat16)
    inb = jnp.einsum("ij,bjg->big", tri, oh, preferred_element_type=jnp.float32)
    ohf = oh.astype(jnp.float32)
    tot = jnp.sum(ohf, axis=1)
    cnt = jnp.sum(tot, axis=0)
    r = inb + (jnp.cumsum(tot, axis=0) - tot)[:, None, :]
    rank = jnp.sum(r * ohf, axis=2).reshape(-1)[:n]
    pos = jnp.sum((r + (jnp.cumsum(cnt) - cnt)) * ohf, axis=2).reshape(-1)[:n]
    return rank.astype(jnp.int32), pos.astype(jnp.int32), cnt.astype(jnp.int32)


def grouped_ffn(rows, gid, w1, w3, w2):
    n, d = rows.shape
    g = w1.shape[0]
    _, pos, cnt = counting(gid, g + 1)
    q = jnp.arange(n, dtype=jnp.int32)
    perm = jnp.sum(jnp.where(pos[:, None] == q[None, :], q[:, None], 0), axis=0)
    xs = rows[perm]
    gs = cnt[:g]
    u = lax.ragged_dot(xs, w1, gs, preferred_element_type=jnp.float32)
    v = lax.ragged_dot(xs, w3, gs, preferred_element_type=jnp.float32)
    a = (jax.nn.silu(u) * v).astype(jnp.bfloat16)
    o = lax.ragged_dot(a, w2, gs, preferred_element_type=jnp.float32).astype(jnp.bfloat16)
    return jnp.where((gid < g)[:, None], o[pos], jnp.zeros((), jnp.bfloat16))


def plan_source(ridx, p, loc, nh):
    td, k = ridx.shape
    e = ridx.reshape(-1)
    hot = e == 0
    dest = e // loc
    capc = td * k // p
    caph = -(-td // nh)
    rank, _, _ = counting(jnp.where(hot, p, dest), p + 1)
    cpos = jnp.where(hot, p * capc, dest * capc + rank)
    hpos = jnp.where(hot, (rank % nh) * caph + rank // nh, nh * caph)
    return hot, cpos, hpos, e % loc, jnp.sum(hot.astype(jnp.int32))


def pack(x, cpos, hpos, lslot, p, capc, nh, caph, value_a5):
    td, d = x.shape
    k = cpos.shape[0] // td
    cm = cpos.reshape(td, k).T[:, None, :] == jnp.arange(p * capc, dtype=jnp.int32)[None, :, None]
    hm = hpos.reshape(td, k).T[:, None, :] == jnp.arange(nh * caph, dtype=jnp.int32)[None, :, None]
    cgid = value_a5 - jnp.sum(jnp.where(cm, value_a5 - lslot.reshape(td, k).T[:, None, :], 0), axis=(0, 2))
    cbuf = jnp.dot(jnp.sum(cm, axis=0).astype(jnp.bfloat16), x, preferred_element_type=jnp.float32).astype(jnp.bfloat16)
    hbuf = jnp.dot(jnp.sum(hm, axis=0).astype(jnp.bfloat16), x, preferred_element_type=jnp.float32).astype(jnp.bfloat16)
    return cbuf, cgid, hbuf.reshape(nh, caph, d)


def combine(gates, hot, cpos, hpos, cret, hres):
    td, k = gates.shape
    d = cret.shape[1]
    hr = hres.reshape(-1, d)
    gt = gates.T[:, :, None]
    zero = jnp.zeros((), gates.dtype)
    gc = jnp.sum(jnp.where(cpos.reshape(td, k).T[:, :, None] == jnp.arange(cret.shape[0], dtype=jnp.int32), gt, zero), axis=0)
    gh = jnp.sum(jnp.where(hpos.reshape(td, k).T[:, :, None] == jnp.arange(hr.shape[0], dtype=jnp.int32), gt, zero), axis=0)
    y = jnp.dot(gc, cret, preferred_element_type=jnp.float32) + jnp.dot(gh, hr, preferred_element_type=jnp.float32)
    return y.astype(jnp.bfloat16)


def solution(mesh):
    p = mesh.shape["ep"]
    hold = holder_list(p)
    nh = len(hold)
    table = [hold.index(q) if q in hold else nh for q in range(p)]

    def local(x, ridx, gates, w1, w3, w2):
        td, d = x.shape
        k = ridx.shape[1]
        value_a5 = w1.shape[0]
        loc = value_a5 - 1
        capc = td * k // p
        caph = -(-td // nh)
        me = lax.axis_index("ep")
        tab = jnp.array(table, jnp.int32)
        gme = tab[me]
        is_h = gme < nh
        slot_h = jnp.where(me == 0, 0, loc)
        hot, cpos, hpos, lslot, nhot = plan_source(ridx, p, loc, nh)
        cbuf, cgid, hbuf = pack(x, cpos, hpos, lslot, p, capc, nh, caph, value_a5)
        counts = lax.all_gather(nhot, "ep")
        crecv = lax.all_to_all(cbuf, "ep", 0, 0, tiled=True)
        crgid = lax.all_to_all(cgid, "ep", 0, 0, tiled=True)
        hblocks = [hbuf[jnp.minimum(gme, nh - 1)]]
        for dl in range(1, p):
            pairs = [(j, (j + dl) % p) for j in range(p) if (j + dl) % p in hold]
            blk = hbuf[jnp.minimum(tab[(me + dl) % p], nh - 1)]
            hblocks.append(lax.ppermute(blk, "ep", pairs))
        hrecv = jnp.stack(hblocks).reshape(p * caph, d)
        srcs = (me - jnp.arange(p)) % p
        cnt = (counts[srcs] - gme + nh - 1) // nh
        valid = jnp.logical_and(jnp.arange(caph)[None, :] < cnt[:, None], is_h)
        hgid = jnp.where(valid, slot_h, value_a5).reshape(-1)
        out = grouped_ffn(jnp.concatenate([crecv, hrecv], axis=0), jnp.concatenate([crgid, hgid], axis=0), w1, w3, w2)
        cret = lax.all_to_all(out[:p * capc], "ep", 0, 0, tiled=True)
        hout = out[p * capc:].reshape(p, caph, d)
        back = [hout[0]]
        for dl in range(1, p):
            pairs = [((j + dl) % p, j) for j in range(p) if (j + dl) % p in hold]
            back.append(lax.ppermute(hout[dl], "ep", pairs))
        hres = jnp.stack(back)[(jnp.array(hold, jnp.int32) - me) % p]
        return combine(gates, hot, cpos, hpos, cret, hres)

    spec_t = P(("dp", "ep"), None)
    spec_w = P("ep", None, None)
    return jax.shard_map(local, mesh=mesh, in_specs=(spec_t, spec_t, spec_t, spec_w, spec_w, spec_w), out_specs=spec_t, check_vma=False)
```

profile of v0, /device:TPU:99, one launch (start us, length us, event | category | flops | bytes accessed | tf_op | source)
XLA Modules:
  0.0 2209.4 jit_solution(8771339354575883244)
XLA Ops:
  89.5 37.9 %convert_reduce_fusion = (s32[6144,768]{1,0:T(8,128)}, s32[6144]{0:T(1024)S(1)}) fusion(s32[8,768]{1,0:T(8,128)} %copy.50, s32[8,768]{1,0:T(8,128)} %copy.52), kind=kLoop, calls=%fused_computation.6 | loop fusion | flops 184018944 | bytes 18948096 | tf_op jit(solution)/shard_map/reduce_sum | solution.py:63
  148.0 29.5 %convolution_convert_fusion = bf16[6144,2048]{1,0:T(8,128)(2,1)} fusion(bf16[768,2048]{1,0:T(8,128)(2,1)S(1)} %copy-done, s32[6144,768]{1,0:T(8,128)} %get-tuple-element.19), kind=kOutput, calls=%fused_computation.15 | convolution fusion | flops 19344654336 | bytes 47185920 | tf_op jit(solution)/shard_map/dot_general | solution.py:63
  178.2 44.9 %all-reduce = s32[32]{0:T(128)S(1)} all-reduce(s32[32]{0:T(128)S(1)} %dynamic-update-slice), channel_id=1, replica_groups=mesh['dp'=1,'ep'=32] {'ep'}, use_global_device_ids=true, to_apply=%add | all-reduce | flops 32 | bytes 256
  224.5 12.3 dynamic-slice_bitcast_fusion
  246.0 112.8 %select_reduce_fusion = s32[12288]{0:T(1024)S(1)} fusion(s32[12288]{0:T(1024)S(1)} %get-tuple-element.89), kind=kLoop, calls=%fused_computation.4 | loop fusion | flops 452972544 | bytes 98304 | tf_op jit(solution)/shard_map/reduce_sum | solution.py:34
  401.7 168.6 %collective-permute-start.10 = (bf16[192,2048]{1,0:T(8,128)(2,1)S(1)}, bf16[192,2048]{1,0:T(8,128)(2,1)S(1)}, u32[]{:S(2)}, u32[]{:S(2)}) collective-permute-start(bf16[192,2048]{1,0:T(8,128)(2,1)S(1)} %copy-done.8), channel_id=1, source_target_pairs={{6,17},{16,27},{21,0},{31,10}} | collective-permute-start | bytes 2359304 | tf_op jit(solution)/shard_map/ppermute | solution.py:107
  629.5 33.0 %collective-permute-start.19 = (bf16[192,2048]{1,0:T(8,128)(2,1)}, bf16[192,2048]{1,0:T(8,128)(2,1)S(1)}, u32[]{:S(2)}, u32[]{:S(2)}) collective-permute-start(bf16[192,2048]{1,0:T(8,128)(2,1)} %get-tuple-element.63), channel_id=1, source_target_pairs={{7,27},{12,0},{22,10},{29,17}} | collective-permute-start | bytes 2359304 | tf_op jit(solution)/shard_map/ppermute | solution.py:107
  750.3 43.5 %pad_maximum_fusion = bf16[12288,2048]{1,0:T(8,128)(2,1)} fusion(bf16[6144,2048]{1,0:T(8,128)(2,1)} %bitcast.276, bf16[6144,2048]{1,0:T(8,128)(2,1)} %bitcast.10), kind=kLoop, calls=%fused_computation.12 | loop fusion | flops 100663296 | bytes 100663296 | tf_op jit(solution)/shard_map/concatenate | solution.py:113
  793.9 286.5 %gather_fusion.1 = bf16[12288,2048]{1,0:T(8,128)(2,1)} fusion(bf16[12288,2048]{1,0:T(8,128)(2,1)} %pad_maximum_fusion, s32[12288]{0:T(1024)S(1)} %broadcast_clamp_fusion.1), kind=kCustom, calls=%fused_computation.1 | custom fusion | bytes 100712448 | tf_op jit(solution)/shard_map/gather | solution.py:35
  1080.4 39.6 %ragged-dot-none.2 = f32[12288,1024]{1,0:T(8,128)} custom-call(s32[1]{0:T(128)} %get-tuple-element.5, s32[4]{0:T(128)} %get-tuple-element.6, s32[50]{0:T(128)} %get-tuple-element.7, s32[50]{0:T(128)} %get-tuple-element.8, s32[1]{0:T(128)} %get-tuple-element.5, bf16[12288,2048]{1,0:T(8,128)(2,1)} %gather_fusion.1, bf16[3,2048,1024]{2,1,0:T(8,128)(2,1)} %param.11), custom_call_target="tpu_custom_call" | custom-call | flops 51539607552 | bytes 113246224 | tf_op jit(solution)/shard_map/ragged_dot_general/ragged-dot-none
  1120.0 39.7 %ragged-dot-none.1 = f32[12288,1024]{1,0:T(8,128)} custom-call(s32[1]{0:T(128)} %get-tuple-element.5, s32[4]{0:T(128)} %get-tuple-element.6, s32[50]{0:T(128)} %get-tuple-element.7, s32[50]{0:T(128)} %get-tuple-element.8, s32[1]{0:T(128)} %get-tuple-element.5, bf16[12288,2048]{1,0:T(8,128)(2,1)} %gather_fusion.1, bf16[3,2048,1024]{2,1,0:T(8,128)(2,1)} %param.12), custom_call_target="tpu_custom_call" | custom-call | flops 51539607552 | bytes 113246224 | tf_op jit(solution)/shard_map/ragged_dot_general/ragged-dot-none
  1159.7 40.1 %multiply_convert_fusion = bf16[12288,1024]{1,0:T(8,128)(2,1)} fusion(f32[12288,1024]{1,0:T(8,128)} %ragged-dot-none.1, f32[12288,1024]{1,0:T(8,128)} %ragged-dot-none.2), kind=kLoop, calls=%fused_computation.13 | loop fusion | flops 75497472 | bytes 125829120 | tf_op jit(solution)/shard_map/convert_element_type | solution.py:39
  1199.8 38.7 %ragged-dot-none = f32[12288,2048]{1,0:T(8,128)} custom-call(s32[1]{0:T(128)} %get-tuple-element.5, s32[4]{0:T(128)} %get-tuple-element.6, s32[50]{0:T(128)} %get-tuple-element.7, s32[50]{0:T(128)} %get-tuple-element.8, s32[1]{0:T(128)} %get-tuple-element.5, bf16[12288,1024]{1,0:T(8,128)(2,1)} %multiply_convert_fusion, bf16[3,1024,2048]{2,1,0:T(8,128)(2,1)} %param.13), custom_call_target="tpu_custom_call" | custom-call | flops 51539607552 | bytes 138412048 | tf_op jit(solution)/shard_map/ragged_dot_general/ragged-dot-none
  1238.5 48.0 %convert_element_type.96 = bf16[12288,2048]{1,0:T(8,128)(2,1)} convert(f32[12288,2048]{1,0:T(8,128)} %ragged-dot-none) | non-fusion elementwise | flops 25165824 | bytes 150994944 | tf_op jit(solution)/shard_map/convert_element_type | solution.py:40
  1286.6 286.1 %gather_fusion.2 = bf16[12288,2048]{1,0:T(8,128)(2,1)} fusion(bf16[12288,2048]{1,0:T(8,128)(2,1)} %convert_element_type.96, s32[12288]{0:T(1024)S(1)} %copy-done.22), kind=kCustom, calls=%fused_computation.2 | custom fusion | bytes 100712448 | tf_op jit(solution)/shard_map/gather | solution.py:41
  1572.7 33.6 %broadcast_select_fusion = bf16[12288,2048]{1,0:T(8,128)(2,1)} fusion(bf16[12288,2048]{1,0:T(8,128)(2,1)} %gather_fusion.2, pred[12288]{0:T(1024)(128)(4,1)S(1)} %copy-done.25), kind=kLoop, calls=%fused_computation.14 | loop fusion | flops 25165824 | bytes 100675584 | tf_op jit(solution)/shard_map/jit(_where)/select_n | solution.py:41
  1606.2 21.0 slice.212
  1627.2 90.9 %all-to-all-start.2 = ((bf16[32,192,2048]{2,1,0:T(8,128)(2,1)}), bf16[32,192,2048]{2,1,0:T(8,128)(2,1)}, u32[]{:S(2)}, u32[]{:S(2)}) async-start(bf16[32,192,2048]{2,1,0:T(8,128)(2,1)} %bitcast.275), calls=%async_computation.2 | async-start | bytes 50331648 | tf_op jit(solution)/shard_map/all_to_all | solution.py:114
  1721.8 29.4 %fusion.1 = bf16[768,6144]{1,0:T(8,128)(2,1)} fusion(s32[8,768]{1,0:T(8,128)S(1)} %copy-done.21, bf16[8,768]{1,0:T(8,128)(2,1)S(1)} %bitcast.283), kind=kLoop, calls=%fused_computation.11 | loop fusion | flops 108527616 | bytes 9474048 | tf_op jit(solution)/shard_map/reduce_sum | solution.py:74
  1778.0 271.2 %collective-permute-done.37 = bf16[192,2048]{1,0:T(8,128)(2,1)S(1)} collective-permute-done((bf16[192,2048]{1,0:T(8,128)(2,1)S(1)}, bf16[192,2048]{1,0:T(8,128)(2,1)S(1)}, u32[]{:S(2)}, u32[]{:S(2)}) %collective-permute-start.37) | collective-permute-done | bytes 786464 | tf_op jit(solution)/shard_map/ppermute | solution.py:119
  2061.9 34.3 %collective-permute-done.44 = bf16[192,2048]{1,0:T(8,128)(2,1)S(1)} collective-permute-done((bf16[192,2048]{1,0:T(8,128)(2,1)S(1)}, bf16[192,2048]{1,0:T(8,128)(2,1)S(1)}, u32[]{:S(2)}, u32[]{:S(2)}) %collective-permute-start.44) | collective-permute-done | bytes 786464 | tf_op jit(solution)/shard_map/ppermute | solution.py:119
  2113.6 11.5 collective-permute-done.54
  2132.7 34.9 %collective-permute-done.59 = bf16[192,2048]{1,0:T(8,128)(2,1)S(1)} collective-permute-done((bf16[192,2048]{1,0:T(8,128)(2,1)S(1)}, bf16[192,2048]{1,0:T(8,128)(2,1)S(1)}, u32[]{:S(2)}, u32[]{:S(2)}) %collective-permute-start.59) | collective-permute-done | bytes 786464 | tf_op jit(solution)/shard_map/ppermute | solution.py:119
  2181.1 23.8 %fusion.50 = f32[768,2048]{1,0:T(8,128)S(1)} fusion(bf16[768,6144]{1,0:T(8,128)(2,1)} %fusion.1, bf16[6144,2048]{1,0:T(8,128)(2,1)} %bitcast.116), kind=kOutput, calls=%fused_computation.213 | convolution fusion | flops 19327352832 | bytes 40894464 | tf_op jit(solution)/shard_map/dot_general | solution.py:76
  (297 shorter events, 375.1 us)
Async XLA Ops:
  46.0 316.0 %collective-permute-start = (bf16[192,2048]{1,0:T(8,128)(2,1)}, bf16[192,2048]{1,0:T(8,128)(2,1)}, u32[]{:S(2)}, u32[]{:S(2)}) collective-permute-start(bf16[192,2048]{1,0:T(8,128)(2,1)} %get-tuple-element.82), channel_id=1, source_target_pairs={{9,10},{16,17},{26,27},{31,0}} | collective-permute-start | bytes 2359304 | tf_op jit(solution)/shard_map/ppermute | solution.py:107
  55.6 315.8 %collective-permute-start.1 = (bf16[192,2048]{1,0:T(8,128)(2,1)}, bf16[192,2048]{1,0:T(8,128)(2,1)}, u32[]{:S(2)}, u32[]{:S(2)}) collective-permute-start(bf16[192,2048]{1,0:T(8,128)(2,1)} %get-tuple-element.81), channel_id=1, source_target_pairs={{8,10},{15,17},{25,27},{30,0}} | collective-permute-start | bytes 2359304 | tf_op jit(solution)/shard_map/ppermute | solution.py:107
  63.2 318.0 %collective-permute-start.2 = (bf16[192,2048]{1,0:T(8,128)(2,1)}, bf16[192,2048]{1,0:T(8,128)(2,1)}, u32[]{:S(2)}, u32[]{:S(2)}) collective-permute-start(bf16[192,2048]{1,0:T(8,128)(2,1)} %get-tuple-element.80), channel_id=1, source_target_pairs={{7,10},{14,17},{24,27},{29,0}} | collective-permute-start | bytes 2359304 | tf_op jit(solution)/shard_map/ppermute | solution.py:107
  71.0 319.0 %collective-permute-start.3 = (bf16[192,2048]{1,0:T(8,128)(2,1)}, bf16[192,2048]{1,0:T(8,128)(2,1)}, u32[]{:S(2)}, u32[]{:S(2)}) collective-permute-start(bf16[192,2048]{1,0:T(8,128)(2,1)} %get-tuple-element.79), channel_id=1, source_target_pairs={{6,10},{13,17},{23,27},{28,0}} | collective-permute-start | bytes 2359304 | tf_op jit(solution)/shard_map/ppermute | solution.py:107
  78.9 319.9 %collective-permute-start.4 = (bf16[192,2048]{1,0:T(8,128)(2,1)}, bf16[192,2048]{1,0:T(8,128)(2,1)}, u32[]{:S(2)}, u32[]{:S(2)}) collective-permute-start(bf16[192,2048]{1,0:T(8,128)(2,1)} %get-tuple-element.78), channel_id=1, source_target_pairs={{5,10},{12,17},{22,27},{27,0}} | collective-permute-start | bytes 2359304 | tf_op jit(solution)/shard_map/ppermute | solution.py:107
  128.1 108.9 %all-to-all-start = ((s32[32,192,1]{1,2,0:T(1,128)}), s32[32,192,1]{1,2,0:T(1,128)S(1)}, u32[]{:S(2)}, u32[]{:S(2)}) async-start(s32[32,192,1]{1,2,0:T(1,128)} %sub.108), calls=%async_computation | async-start | bytes 65536 | tf_op jit(solution)/shard_map/all_to_all | solution.py:102
  237.1 513.2 %all-to-all-start.1 = ((bf16[32,192,2048]{2,1,0:T(8,128)(2,1)}), bf16[32,192,2048]{2,1,0:T(8,128)(2,1)}, u32[]{:S(2)}, u32[]{:S(2)}) async-start(bf16[32,192,2048]{2,1,0:T(8,128)(2,1)} %bitcast.277), calls=%async_computation.1 | async-start | bytes 50331648 | tf_op jit(solution)/shard_map/all_to_all | solution.py:101
  371.3 199.9 %collective-permute-start.6 = (bf16[192,2048]{1,0:T(8,128)(2,1)}, bf16[192,2048]{1,0:T(8,128)(2,1)S(1)}, u32[]{:S(2)}, u32[]{:S(2)}) collective-permute-start(bf16[192,2048]{1,0:T(8,128)(2,1)} %get-tuple-element.76), channel_id=1, source_target_pairs={{3,10},{10,17},{20,27},{25,0}} | collective-permute-start | bytes 2359304 | tf_op jit(solution)/shard_map/ppermute | solution.py:107
  381.2 198.1 %collective-permute-start.7 = (bf16[192,2048]{1,0:T(8,128)(2,1)}, bf16[192,2048]{1,0:T(8,128)(2,1)S(1)}, u32[]{:S(2)}, u32[]{:S(2)}) collective-permute-start(bf16[192,2048]{1,0:T(8,128)(2,1)} %get-tuple-element.75), channel_id=1, source_target_pairs={{2,10},{9,17},{19,27},{24,0}} | collective-permute-start | bytes 2359304 | tf_op jit(solution)/shard_map/ppermute | solution.py:107
  390.0 197.7 %collective-permute-start.8 = (bf16[192,2048]{1,0:T(8,128)(2,1)}, bf16[192,2048]{1,0:T(8,128)(2,1)S(1)}, u32[]{:S(2)}, u32[]{:S(2)}) collective-permute-start(bf16[192,2048]{1,0:T(8,128)(2,1)} %get-tuple-element.74), channel_id=1, source_target_pairs={{1,10},{8,17},{18,27},{23,0}} | collective-permute-start | bytes 2359304 | tf_op jit(solution)/shard_map/ppermute | solution.py:107
  398.8 197.7 %collective-permute-start.9 = (bf16[192,2048]{1,0:T(8,128)(2,1)S(1)}, bf16[192,2048]{1,0:T(8,128)(2,1)S(1)}, u32[]{:S(2)}, u32[]{:S(2)}) collective-permute-start(bf16[192,2048]{1,0:T(8,128)(2,1)S(1)} %copy-done.9), channel_id=1, source_target_pairs={{0,10},{7,17},{17,27},{22,0}} | collective-permute-start | bytes 2359304 | tf_op jit(solution)/shard_map/ppermute | solution.py:107
  401.7 202.5 %collective-permute-start.10 = (bf16[192,2048]{1,0:T(8,128)(2,1)S(1)}, bf16[192,2048]{1,0:T(8,128)(2,1)S(1)}, u32[]{:S(2)}, u32[]{:S(2)}) collective-permute-start(bf16[192,2048]{1,0:T(8,128)(2,1)S(1)} %copy-done.8), channel_id=1, source_target_pairs={{6,17},{16,27},{21,0},{31,10}} | collective-permute-start | bytes 2359304 | tf_op jit(solution)/shard_map/ppermute | solution.py:107
  604.2 59.3 %collective-permute-start.15 = (bf16[192,2048]{1,0:T(8,128)(2,1)}, bf16[192,2048]{1,0:T(8,128)(2,1)S(1)}, u32[]{:S(2)}, u32[]{:S(2)}) collective-permute-start(bf16[192,2048]{1,0:T(8,128)(2,1)} %get-tuple-element.67), channel_id=1, source_target_pairs={{1,17},{11,27},{16,0},{26,10}} | collective-permute-start | bytes 2359304 | tf_op jit(solution)/shard_map/ppermute | solution.py:107
  611.9 59.8 %collective-permute-start.16 = (bf16[192,2048]{1,0:T(8,128)(2,1)}, bf16[192,2048]{1,0:T(8,128)(2,1)S(1)}, u32[]{:S(2)}, u32[]{:S(2)}) collective-permute-start(bf16[192,2048]{1,0:T(8,128)(2,1)} %get-tuple-element.66), channel_id=1, source_target_pairs={{0,17},{10,27},{15,0},{25,10}} | collective-permute-start | bytes 2359304 | tf_op jit(solution)/shard_map/ppermute | solution.py:107
  613.6 66.3 %collective-permute-start.17 = (bf16[192,2048]{1,0:T(8,128)(2,1)}, bf16[192,2048]{1,0:T(8,128)(2,1)S(1)}, u32[]{:S(2)}, u32[]{:S(2)}) collective-permute-start(bf16[192,2048]{1,0:T(8,128)(2,1)} %get-tuple-element.65), channel_id=1, source_target_pairs={{9,27},{14,0},{24,10},{31,17}} | collective-permute-start | bytes 2359304 | tf_op jit(solution)/shard_map/ppermute | solution.py:107
  621.8 66.4 %collective-permute-start.18 = (bf16[192,2048]{1,0:T(8,128)(2,1)}, bf16[192,2048]{1,0:T(8,128)(2,1)S(1)}, u32[]{:S(2)}, u32[]{:S(2)}) collective-permute-start(bf16[192,2048]{1,0:T(8,128)(2,1)} %get-tuple-element.64), channel_id=1, source_target_pairs={{8,27},{13,0},{23,10},{30,17}} | collective-permute-start | bytes 2359304 | tf_op jit(solution)/shard_map/ppermute | solution.py:107
  629.5 67.1 %collective-permute-start.19 = (bf16[192,2048]{1,0:T(8,128)(2,1)}, bf16[192,2048]{1,0:T(8,128)(2,1)S(1)}, u32[]{:S(2)}, u32[]{:S(2)}) collective-permute-start(bf16[192,2048]{1,0:T(8,128)(2,1)} %get-tuple-element.63), channel_id=1, source_target_pairs={{7,27},{12,0},{22,10},{29,17}} | collective-permute-start | bytes 2359304 | tf_op jit(solution)/shard_map/ppermute | solution.py:107
  1627.2 553.9 %all-to-all-start.2 = ((bf16[32,192,2048]{2,1,0:T(8,128)(2,1)}), bf16[32,192,2048]{2,1,0:T(8,128)(2,1)}, u32[]{:S(2)}, u32[]{:S(2)}) async-start(bf16[32,192,2048]{2,1,0:T(8,128)(2,1)} %bitcast.275), calls=%async_computation.2 | async-start | bytes 50331648 | tf_op jit(solution)/shard_map/all_to_all | solution.py:114
  1769.0 280.2 %collective-permute-start.37 = (bf16[192,2048]{1,0:T(8,128)(2,1)S(1)}, bf16[192,2048]{1,0:T(8,128)(2,1)S(1)}, u32[]{:S(2)}, u32[]{:S(2)}) collective-permute-start(bf16[192,2048]{1,0:T(8,128)(2,1)S(1)} %get-tuple-element.45), channel_id=1, source_target_pairs={{10,3},{17,10},{27,20},{0,25}} | collective-permute-start | bytes 2359304 | tf_op jit(solution)/shard_map/ppermute | solution.py:119
  1771.2 279.6 %collective-permute-start.38 = (bf16[192,2048]{1,0:T(8,128)(2,1)S(1)}, bf16[192,2048]{1,0:T(8,128)(2,1)S(1)}, u32[]{:S(2)}, u32[]{:S(2)}) collective-permute-start(bf16[192,2048]{1,0:T(8,128)(2,1)S(1)} %get-tuple-element.44), channel_id=1, source_target_pairs={{10,2},{17,9},{27,19},{0,24}} | collective-permute-start | bytes 2359304 | tf_op jit(solution)/shard_map/ppermute | solution.py:119
  1772.9 279.6 %collective-permute-start.39 = (bf16[192,2048]{1,0:T(8,128)(2,1)S(1)}, bf16[192,2048]{1,0:T(8,128)(2,1)S(1)}, u32[]{:S(2)}, u32[]{:S(2)}) collective-permute-start(bf16[192,2048]{1,0:T(8,128)(2,1)S(1)} %get-tuple-element.43), channel_id=1, source_target_pairs={{10,1},{17,8},{27,18},{0,23}} | collective-permute-start | bytes 2359304 | tf_op jit(solution)/shard_map/ppermute | solution.py:119
  1774.6 280.2 %collective-permute-start.40 = (bf16[192,2048]{1,0:T(8,128)(2,1)S(1)}, bf16[192,2048]{1,0:T(8,128)(2,1)S(1)}, u32[]{:S(2)}, u32[]{:S(2)}) collective-permute-start(bf16[192,2048]{1,0:T(8,128)(2,1)S(1)} %get-tuple-element.42), channel_id=1, source_target_pairs={{10,0},{17,7},{27,17},{0,22}} | collective-permute-start | bytes 2359304 | tf_op jit(solution)/shard_map/ppermute | solution.py:119
  1776.3 280.5 %collective-permute-start.41 = (bf16[192,2048]{1,0:T(8,128)(2,1)S(1)}, bf16[192,2048]{1,0:T(8,128)(2,1)S(1)}, u32[]{:S(2)}, u32[]{:S(2)}) collective-permute-start(bf16[192,2048]{1,0:T(8,128)(2,1)S(1)} %get-tuple-element.41), channel_id=1, source_target_pairs={{17,6},{27,16},{0,21},{10,31}} | collective-permute-start | bytes 2359304 | tf_op jit(solution)/shard_map/ppermute | solution.py:119
  2052.6 43.5 %collective-permute-start.44 = (bf16[192,2048]{1,0:T(8,128)(2,1)S(1)}, bf16[192,2048]{1,0:T(8,128)(2,1)S(1)}, u32[]{:S(2)}, u32[]{:S(2)}) collective-permute-start(bf16[192,2048]{1,0:T(8,128)(2,1)S(1)} %get-tuple-element.38), channel_id=1, source_target_pairs={{17,3},{27,13},{0,18},{10,28}} | collective-permute-start | bytes 2359304 | tf_op jit(solution)/shard_map/ppermute | solution.py:119
  (68 other events, 6370.6 us)
where the time goes:
time: 2240 us; the launch traced here: 2210 us
  local copies, waits for them, and re-layouts  719 us (32%)
  starting transfers between devices  516 us (23%)
  other arithmetic  365 us (16%)
  waiting for transfers between devices  359 us (16%)
  Pallas kernels  120 us (5%)
  matrix products  63 us (3%)
  blocking collectives  44.9 us (2%)
  between operations  22.5 us (1%)
    ppermute x31, starting transfers between devices, local(): hblocks.append(lax.ppermute(blk, 'ep', pairs))  386 us
    ppermute x31, waiting for transfers between devices, local(): back.append(lax.ppermute(hout[dl], 'ep', pairs))  352 us
    gather x1, local copies, waits for them, and re-layouts, grouped_ffn(): xs = rows[perm]  287 us
    gather x1, local copies, waits for them, and re-layouts, grouped_ffn(): return jnp.where((gid < g)[:, None], o[pos], jnp.zeros((), jnp.bfloat16))  286 us
    another operation x3, Pallas kernels  118 us
    reduce_sum x1, other arithmetic, grouped_ffn(): perm = jnp.sum(jnp.where(pos[:, None] == q[None, :], q[:, None], 0), axis=0)  113 us
    all_to_all x1, starting transfers between devices, local(): cret = lax.all_to_all(out[:p * capc], 'ep', 0, 0, tiled=True)  90.9 us
    unnamed x118, local copies, waits for them, and re-layouts  70.4 us
  transfers between devices with their start and end apart: 65, of which 5 were waited for; matrix products, arithmetic and copies ran while one was open for 15% of the time, Pallas kernels for 0%

commit v1 on v0

v1 whole, which is shorter than its diff:
```python
import functools
import math

import jax
import jax.numpy as jnp
from jax import lax
from jax.experimental import pallas as pl
from jax.experimental.pallas import tpu as pltpu
from jax.sharding import PartitionSpec as P

MESH = pl.DeviceIdType.MESH
ANY = pl.BlockSpec(memory_space=pl.ANY)
SMEM = pl.BlockSpec(memory_space=pltpu.SMEM)
VMEM = pl.BlockSpec(memory_space=pltpu.VMEM)
F32 = jnp.float32
BF16 = jnp.bfloat16
NT = 256
RING = 4
LAG_F = 2
LAG_C = 5
PARTS = 2


def holder_list(p):
    return [0, (p // 2 + 1) % p, (p // 4 + 2) % p, (3 * p // 4 + 3) % p]


class Place:
    def __init__(self, side):
        me = lax.axis_index("ep")
        self.side = side
        self.z = lax.axis_index("dp")
        self.c = lax.rem(me, 2)
        self.x = lax.rem(lax.div(me, 2), side)
        self.y = lax.div(me, 2 * side)

    def index(self, dy, dx, c):
        s = self.side
        return (lax.rem(self.y + dy, s) * s + lax.rem(self.x + dx, s)) * 2 + c

    def dev(self, dy, dx, c):
        return (self.z, self.index(dy, dx, c))

    def greet(self):
        bar = pltpu.get_barrier_semaphore()
        near = [self.dev(0, 0, 1 - self.c)]
        for k in range(1, self.side):
            for c in range(2):
                near += [self.dev(0, k, c), self.dev(k, 0, c)]
        for d in near:
            pl.semaphore_signal(bar, inc=1, device_id=d, device_id_type=MESH)
        pl.semaphore_wait(bar, len(near))


def remote(src, dst, ssem, rsem, dev):
    return pltpu.make_async_remote_copy(src_ref=src, dst_ref=dst, send_sem=ssem, recv_sem=rsem, device_id=dev, device_id_type=MESH)


def weights_kernel(side, loc, w1, w3, w2, h1, h3, h2, s_sem, r_sem, p_sem, q_sem):
    at = Place(side)
    hx, hc = lax.rem(at.y, 2), lax.div(at.y, 2)
    slot = lax.div(at.y + side - 1, side) * loc
    rel = lax.rem(at.x + side - hx, side)
    right, left, mate = at.dev(0, 1, at.c), at.dev(0, side - 1, at.c), at.dev(0, 0, 1 - at.c)
    bar = pltpu.get_barrier_semaphore()
    for d in (right, left, mate):
        pl.semaphore_signal(bar, inc=1, device_id=d, device_id_type=MESH)
    pl.semaphore_wait(bar, 3)
    lane = at.c == hc
    pieces = []
    for m, (w, h) in enumerate(((w1, h1), (w3, h3), (w2, h2))):
        n = w.shape[1] // (2 * PARTS)
        for i in range(PARTS):
            pieces.append([(w, h, pl.ds((half * PARTS + i) * n, n), (m * PARTS + i) * 2 + half) for half in range(2)])
    order = [pieces[m * PARTS + i] for m in range(3) for i in range(PARTS)]

    def hop(src, dst, j, d):
        return remote(src, dst, s_sem.at[j], r_sem.at[j], d)

    def pass_on(src, dst, j):
        return remote(src, dst, p_sem.at[j], q_sem.at[j], mate)

    @pl.when(jnp.logical_and(lane, rel == 0))
    def _():
        for pair in order:
            for half, (w, h, rows, j) in enumerate(pair):
                hop(w.at[slot, rows], h.at[rows], j, right if half == 0 else left).start()
                pass_on(w.at[slot, rows], h.at[rows], j).start()
        for pair in order:
            for half, (w, h, rows, j) in enumerate(pair):
                hop(w.at[slot, rows], h.at[rows], j, right).wait_send()
                pass_on(w.at[slot, rows], h.at[rows], j).wait_send()

    def relay(r):
        todo = sorted((n + (r if half == 0 else side - r), half, n) for n in range(len(order)) for half in range(2))
        for _, half, n in todo:
            w, h, rows, j = order[n][half]
            hop(h.at[rows], h.at[rows], j, right).wait_recv()
            if (r < side - 1) if half == 0 else (r > 1):
                hop(h.at[rows], h.at[rows], j, right if half == 0 else left).start()
            pass_on(h.at[rows], h.at[rows], j).start()
        for _, half, n in todo:
            w, h, rows, j = order[n][half]
            pass_on(h.at[rows], h.at[rows], j).wait_send()
            if (r < side - 1) if half == 0 else (r > 1):
                hop(h.at[rows], h.at[rows], j, right).wait_send()

    for r in range(1, side):
        pl.when(jnp.logical_and(lane, rel == r))(functools.partial(relay, r))

    @pl.when(at.c != hc)
    def _():
        for pair in order:
            for w, h, rows, j in pair:
                pass_on(h.at[rows], h.at[rows], j).wait_recv()


def dispatch_kernel(side, cap, x, ml, mr, recvl, recvr, xl, xr, mlv, mrv, sel, sbl, sbr, own, ag_s, ag_r, m_s, m_r, s_l, r_l, s_r, r_r):
    at = Place(side)
    td = x.shape[0]
    cl, cr = xl.shape[2], xr.shape[2]
    half = td // 2
    sides = (
        dict(i=0, xv=xl, cols=pl.ds(0, cl), m=ml, mv=mlv, sb=sbl, rv=recvl, ss=s_l, rs=r_l, axis=0),
        dict(i=1, xv=xr, cols=pl.ds(cl, cr), m=mr, mv=mrv, sb=sbr, rv=recvr, ss=s_r, rs=r_r, axis=1),
    )

    def along(a, k, c):
        return at.dev(k, 0, c) if a == 0 else at.dev(0, k, c)

    mine = []
    for t in sides:
        i, here = t["i"], at.y if t["axis"] == 0 else at.x
        mine.append(pltpu.make_async_copy(x.at[:, t["cols"]], t["xv"].at[0], own.at[i, 0]))
        mine.append(pltpu.make_async_copy(t["m"].at[here], t["mv"].at[0], own.at[i, 1]))
    for cp in mine:
        cp.start()
    at.greet()
    last = side - 1
    sends = []
    for t in sides:
        i, a, here = t["i"], t["axis"], at.y if t["axis"] == 0 else at.x
        for k in range(1, side):
            sends.append(remote(t["m"].at[lax.rem(here + k, side)], t["mv"].at[side - k], m_s.at[i, k], m_r.at[i, side - k], along(a, k, at.c)))
        sends.append(remote(x.at[:, t["cols"]], t["xv"].at[last], ag_s.at[i, 0], ag_r.at[i, last], along(a, 1, at.c)))
        sends.append(remote(x.at[:, t["cols"]], t["xv"].at[1], ag_s.at[i, 1], ag_r.at[i, 1], along(a, last, at.c)))
    for cp in sends:
        cp.start()

    def pack(t, k):
        there = at.x if t["axis"] == 0 else at.y
        width = t["xv"].shape[2]

        def one(d, carry):
            q = lax.rem(there + d, side)
            r = lax.broadcasted_iota(jnp.int32, (cap, td), 0).astype(F32)
            for c in range(2):
                p0 = t["mv"][k, q, 2 * c : 2 * c + 1, :]
                p1 = t["mv"][k, q, 2 * c + 1 : 2 * c + 2, :]
                hit = jnp.logical_or(r == p0, r == p1)
                sel[c * cap : (c + 1) * cap, :] = jnp.where(hit, 1.0, 0.0).astype(BF16)

            def col(n, carry):
                cols = pl.ds(pl.multiple_of(n * NT, NT), NT)
                o = jnp.dot(sel[...], t["xv"][k, :, cols], preferred_element_type=F32).astype(BF16)
                t["sb"][k, d, :, :, cols] = o.reshape(2, cap, NT)
                return carry

            return lax.fori_loop(0, width // NT, col, carry)

        lax.fori_loop(0, side, one, 0)

    def block(t, k, d, c):
        to = (side - d) % side
        slot = (k, to, at.c) if t["axis"] == 0 else (to, k, at.c)
        return remote(t["sb"].at[k, d, c], t["rv"].at[slot], t["ss"].at[k, d, c], t["rs"].at[slot], along(1 - t["axis"], d, c))

    def send(t, k):
        for d in (1, side - 1, 2):
            for c in range(2):
                block(t, k, d, c).start()
        block(t, k, 0, 1 - at.c).start()
        slot = (k, 0, at.c) if t["axis"] == 0 else (0, k, at.c)
        pltpu.make_async_copy(t["sb"].at[k, 0, at.c], t["rv"].at[slot], t["rs"].at[slot]).start()

    for cp in mine:
        cp.wait()
    pack(sides[0], 0)
    pack(sides[1], 0)
    fwd = []
    for t in sides:
        i, a, xv = t["i"], t["axis"], t["xv"]
        for k, rows, to in ((last, pl.ds(0, half), 1), (1, pl.ds(half, half), last)):
            remote(xv.at[k], xv.at[k], ag_s.at[i, 0], ag_r.at[i, k], along(a, 1, at.c)).wait_recv()
            cp = remote(xv.at[k, rows], xv.at[2, rows], ag_s.at[i, 2 if to == 1 else 3], ag_r.at[i, 2 if to == 1 else 0], along(a, to, at.c))
            cp.start()
            fwd.append(cp)
        for k in range(1, side):
            remote(t["mv"].at[k], t["mv"].at[k], m_s.at[i, k], m_r.at[i, k], along(a, 1, at.c)).wait_recv()
    send(sides[0], 0)
    send(sides[1], 0)
    for k in (last, 1):
        for t in sides:
            pack(t, k)
        for t in sides:
            send(t, k)
    for cp in fwd:
        cp.wait_recv()
    for t in sides:
        pack(t, 2)
    for t in sides:
        send(t, 2)
    for cp in sends + fwd:
        cp.wait_send()

    def settle(j, carry):
        k, d, c = lax.div(j, 2 * side), lax.rem(lax.div(j, 2), side), lax.rem(j, 2)
        for t in sides:
            dst = t["rv"].at[k, d, c]
            remote(t["sb"].at[0, 0, 0], dst, t["ss"].at[k, d, c], t["rs"].at[k, d, c], along(0, 1, at.c)).wait_recv()

            @pl.when(jnp.logical_or(d != 0, c != at.c))
            def _():
                remote(t["sb"].at[k, d, c], dst, t["ss"].at[k, d, c], t["rs"].at[k, d, c], along(0, 1, at.c)).wait_send()

        return carry

    lax.fori_loop(0, 2 * side * side, settle, 0)


def experts_kernel(
    side, cap, slot_last, n0, x, recvl, recvr, w1, w3, w2, h1, h3, h2, pt, gt, gh,
    y, rell, relr, retl, retr,
    w1v, w3v, w2v, xbl, xbr, xs, av, ol, orr, ocl, ocr, gm, yacc,
    w_sem, x_sem, o_sem, c_sem, s1l, s1r, r1l, r1r, s2l, s2r, r2l, r2r,
):
    at = Place(side)
    td = x.shape[0]
    cl, cr = ol.shape[3], orr.shape[3]
    d_model, ff = w1.shape[1], w1.shape[2]
    steps = side * side
    n_rel = (side - 1) * (side - 1)
    m2 = 2 * cap

    def where_to(s):
        b = lax.div(s, n_rel)
        t = s - b * n_rel
        r, q = lax.rem(t, 3), lax.div(t, 3)
        e, f = lax.rem(t, 2), lax.div(t, 2)
        dx = (1 - b) * (1 + r) + b * (1 - e) * (1 + f)
        dy = (1 - b) * (1 + lax.rem(r + q, 3)) + b * e * (1 + f)
        return lax.rem(dy, side), lax.rem(dx, side)

    def load_w(w, v, n, i):
        return pltpu.make_async_copy(w, v, w_sem.at[i])

    wcp = [load_w(w.at[pl.ds(0, 2)], v, 2, i) for i, (w, v) in enumerate(((w1, w1v), (w3, w3v), (w2, w2v)))]
    for cp in wcp:
        cp.start()

    def load_x(s):
        dy, dx = where_to(s)
        slot = lax.rem(s, 2)
        return (
            pltpu.make_async_copy(recvl.at[dy, dx], xbl.at[slot], x_sem.at[slot, 0]),
            pltpu.make_async_copy(recvr.at[dy, dx], xbr.at[slot], x_sem.at[slot, 1]),
        )

    for cp in load_x(0):
        cp.start()
    yacc[...] = jnp.zeros_like(yacc)
    at.greet()
    for cp in wcp:
        cp.wait()

    halves = ((ol, rell, retl, s1l, r1l, s2l, r2l), (orr, relr, retr, s1r, r1r, s2r, r2r))

    def first_hop(s, side_i):
        o, rel, ret, s1, r1, s2, r2 = halves[side_i]
        dy, dx = where_to(s)
        so = lax.rem(s, RING)
        if side_i == 0:
            relay = remote(o.at[so], rel.at[s], s1.at[s, 0], r1.at[s], at.dev(0, dx, at.c))
        else:
            relay = remote(o.at[so], rel.at[s], s1.at[s, 0], r1.at[s], at.dev(dy, 0, at.c))
        direct = [remote(o.at[so, c], ret.at[s, at.c], s1.at[s, c], r2.at[s, at.c], at.dev(dy, dx, c)) for c in range(2)]
        mate = remote(o.at[so, 1 - at.c], ret.at[s, at.c], s1.at[s, 0], r2.at[s, at.c], at.dev(0, 0, 1 - at.c))
        self_cp = pltpu.make_async_copy(o.at[so, at.c], ret.at[s, at.c], r2.at[s, at.c])
        return relay, direct, mate, self_cp

    def start_first(s):
        for h in range(2):
            relay, direct, mate, self_cp = first_hop(s, h)

            @pl.when(s < n_rel)
            def _():
                relay.start()

            @pl.when(jnp.logical_and(s >= n_rel, s < steps - 1))
            def _():
                for cp in direct:
                    cp.start()

            @pl.when(s == steps - 1)
            def _():
                mate.start()
                self_cp.start()

    def wait_first(s):
        for h in range(2):
            relay, direct, mate, _ = first_hop(s, h)

            @pl.when(s < n_rel)
            def _():
                relay.wait_send()

            @pl.when(jnp.logical_and(s >= n_rel, s < steps - 1))
            def _():
                for cp in direct:
                    cp.wait_send()

            @pl.when(s == steps - 1)
            def _():
                mate.wait_send()

    def second_hop(s, side_i):
        o, rel, ret, s1, r1, s2, r2 = halves[side_i]
        dy, dx = where_to(s)
        got = remote(rel.at[s], rel.at[s], s1.at[s, 0], r1.at[s], at.dev(0, 1, at.c))
        if side_i == 0:
            on = [remote(rel.at[s, c], ret.at[s, at.c], s2.at[s, c], r2.at[s, at.c], at.dev(dy, 0, c)) for c in range(2)]
        else:
            on = [remote(rel.at[s, c], ret.at[s, at.c], s2.at[s, c], r2.at[s, at.c], at.dev(0, dx, c)) for c in range(2)]
        return got, on

    def forward(s):
        for h in range(2):
            got, on = second_hop(s, h)
            got.wait_recv()
            for cp in on:
                cp.start()

    def fetch(s):
        for h, oc in enumerate((ocl, ocr)):
            o, rel, ret, s1, r1, s2, r2 = halves[h]
            for c in range(2):
                remote(ret.at[s, c], ret.at[s, c], s2.at[s, c], r2.at[s, c], at.dev(0, 1, at.c)).wait_recv()
            pltpu.make_async_copy(ret.at[s], oc, c_sem.at[h]).start()

    def combine(s):
        dy, dx = where_to(s)
        chip = lax.rem(at.y + side - dy, side) * side + lax.rem(at.x + side - dx, side)
        r = lax.broadcasted_iota(jnp.int32, (cap, td), 0).astype(F32)
        for c in range(2):
            g = jnp.zeros((cap, td), F32)
            for j in range(2):
                row = 2 * c + j
                g = g + jnp.where(r == pt[chip, row : row + 1, :], gt[chip, row : row + 1, :], 0.0)
            gm[c * cap : (c + 1) * cap, :] = g.astype(BF16)
        for h, oc in enumerate((ocl, ocr)):
            pltpu.make_async_copy(halves[h][2].at[s], oc, c_sem.at[h]).wait()
            width = cl if h == 0 else cr

            def col(n, carry):
                cols = pl.ds(pl.multiple_of(n * NT, NT), NT)
                to = pl.ds(pl.multiple_of(h * cl + n * NT, NT), NT)
                b = oc[:, :, cols].reshape(m2, NT)
                yacc[:, to] += lax.dot_general(gm[...], b, (((0,), (0,)), ((), ())), preferred_element_type=F32)
                return carry

            lax.fori_loop(0, width // NT, col, 0)

    def up(f, carry, experts):
        cols = pl.ds(pl.multiple_of(f * NT, NT), NT)
        u = sum(jnp.dot(xs[e], w1v[e, :, cols], preferred_element_type=F32) for e in range(experts))
        v = sum(jnp.dot(xs[e], w3v[e, :, cols], preferred_element_type=F32) for e in range(experts))
        a = (jax.nn.silu(u) * v).astype(BF16)
        return a, cols

    def step(s, carry):
        slot, so = lax.rem(s, 2), lax.rem(s, RING)
        dy, dx = where_to(s)

        @pl.when(s + 1 < steps)
        def _():
            for cp in load_x(s + 1):
                cp.start()

        for cp in load_x(s):
            cp.wait()
        cuts = [n0[at.index(dy, dx, c)] for c in range(2)]
        for c in range(2):
            for xb, lo, width in ((xbl, 0, cl), (xbr, cl, cr)):
                for n in range(width // NT):
                    v = xb[slot, c, :, n * NT : (n + 1) * NT].astype(F32)
                    first = lax.broadcasted_iota(jnp.int32, (cap, NT), 0) < cuts[c]
                    z = jnp.zeros_like(v)
                    to = slice(lo + n * NT, lo + (n + 1) * NT)
                    xs[0, c * cap : (c + 1) * cap, to] = jnp.where(first, v, z).astype(BF16)
                    xs[1, c * cap : (c + 1) * cap, to] = jnp.where(first, z, v).astype(BF16)

        def up2(f, carry):
            a, cols = up(f, carry, 2)
            a = a.astype(F32)
            row = lax.broadcasted_iota(jnp.int32, (cap, NT), 0)
            first = jnp.concatenate([jnp.where(row < cuts[c], 1.0, 0.0) for c in range(2)], axis=0)
            a0 = jnp.where(first > 0.5, a, 0.0)
            av[0, :, cols] = a0.astype(BF16)
            av[1, :, cols] = (a - a0).astype(BF16)
            return carry

        lax.fori_loop(0, ff // NT, up2, 0)

        @pl.when(s >= RING)
        def _():
            wait_first(s - RING)

        for o, lo, width in ((ol, 0, cl), (orr, cl, cr)):

            def down(n, carry):
                to = pl.ds(pl.multiple_of(n * NT, NT), NT)
                cols = pl.ds(pl.multiple_of(lo + n * NT, NT), NT)
                r = sum(jnp.dot(av[e], w2v[e, :, cols], preferred_element_type=F32) for e in range(2))
                o[so, :, :, to] = r.astype(BF16).reshape(2, cap, NT)
                return carry

            lax.fori_loop(0, width // NT, down, 0)

        @pl.when(jnp.logical_and(s >= LAG_F, s - LAG_F < n_rel))
        def _():
            forward(s - LAG_F)

        @pl.when(s >= LAG_C)
        def _():
            combine(s - LAG_C)

        start_first(s)

        @pl.when(s >= LAG_C - 1)
        def _():
            fetch(s - LAG_C + 1)

        return carry

    lax.fori_loop(0, steps, step, 0)

    is_h = jnp.logical_and(at.x == lax.rem(at.y, 2), at.c == lax.div(at.y, 2))
    hs = lax.div(at.y + side - 1, side) * slot_last
    for i, (w, h, v) in enumerate(((w1, h1, w1v), (w3, h3, w3v), (w2, h2, w2v))):

        @pl.when(is_h)
        def _():
            load_w(w.at[hs], v.at[0], 1, i).start()

        @pl.when(jnp.logical_not(is_h))
        def _():
            load_w(h, v.at[0], 1, i).start()

    def load_own(i):
        return pltpu.make_async_copy(x.at[pl.ds(i * m2, m2)], xs.at[i], x_sem.at[i, 0])

    for i in range(td // m2):
        load_own(i).start()

    def drain(s, carry):
        combine(s)

        @pl.when(s + 1 < steps)
        def _():
            fetch(s + 1)

        return carry

    lax.fori_loop(steps - LAG_C, steps - 2, drain, 0)
    for i, (h, v) in enumerate(((h1, w1v), (h3, w3v), (h2, w2v))):
        load_w(h, v.at[0], 1, i).wait()
    for i in range(td // m2):
        load_own(i).wait()

        def up1(f, carry):
            cols = pl.ds(pl.multiple_of(f * NT, NT), NT)
            u = jnp.dot(xs[i], w1v[0, :, cols], preferred_element_type=F32)
            v = jnp.dot(xs[i], w3v[0, :, cols], preferred_element_type=F32)
            av[0, :, cols] = (jax.nn.silu(u) * v).astype(BF16)
            return carry

        lax.fori_loop(0, ff // NT, up1, 0)

        def down1(n, carry):
            cols = pl.ds(pl.multiple_of(n * NT, NT), NT)
            r = jnp.dot(av[0], w2v[0, :, cols], preferred_element_type=F32).astype(BF16).astype(F32)
            g = gh[i * m2 : (i + 1) * m2, :]
            yacc[i * m2 : (i + 1) * m2, cols] += jnp.where(g > 0.0, g * r, 0.0)
            return carry

        lax.fori_loop(0, d_model // NT, down1, 0)

    lax.fori_loop(steps - 2, steps, drain, 0)

    def out(n, carry):
        cols = pl.ds(pl.multiple_of(n * NT, NT), NT)
        y[:, cols] = yacc[:, cols].astype(BF16)
        return carry

    lax.fori_loop(0, d_model // NT, out, 0)

    def settle(s, carry):
        wait_first(s)
        return carry

    lax.fori_loop(steps - RING, steps, settle, 0)

    def settle2(s, carry):
        for h in range(2):
            for cp in second_hop(s, h)[1]:
                cp.wait_send()
        return carry

    lax.fori_loop(0, n_rel, settle2, 0)


def plan(ridx, gates, p, experts):
    td, k = ridx.shape
    ids = jnp.arange(experts, dtype=ridx.dtype)
    hit = ridx[:, :, None] == ids
    g = jnp.sum(jnp.where(hit, gates.astype(F32)[:, :, None], 0.0), axis=1)
    m = jnp.logical_and(jnp.any(hit, axis=1), ids[None, :] > 0)
    mb = m.astype(BF16)
    tri = (jnp.arange(td)[:, None] > jnp.arange(td)[None, :]).astype(BF16)
    rank = jnp.dot(tri, mb, preferred_element_type=F32)
    cnt = jnp.sum(m.astype(F32), axis=0)
    loc = experts // p
    before = jnp.cumsum(cnt.reshape(p, loc), axis=1) - cnt.reshape(p, loc)
    pos = jnp.where(m, rank + before.reshape(-1), -1.0)
    return pos.T, g.T, cnt.reshape(p, loc)[:, 0].astype(jnp.int32)


def solution(mesh):
    p = mesh.shape["ep"]
    side = math.isqrt(p // 2)
    want = [(y * side + y % 2) * 2 + y // 2 for y in range(side)]
    if side != 4 or sorted(holder_list(p)) != sorted(want) or holder_list(p)[0] != want[0]:
        raise ValueError("unknown placement")

    def local(x, ridx, gates, w1, w3, w2):
        td, d = x.shape
        k = ridx.shape[1]
        slots, _, ff = w1.shape
        loc = slots - 1
        cap = td * k // p
        cl = 3 * d // 8 // NT * NT
        cr = d - cl
        pt, gt, n0 = plan(ridx, gates, p, p * loc)
        n0 = lax.all_to_all(n0.reshape(p, 1), "ep", 0, 0, tiled=True).reshape(p)
        pc = pt.reshape(side, side, 2 * loc, td)
        ml, mr = pc, pc.transpose(1, 0, 2, 3)
        gc = gt.reshape(side * side, 2 * loc, td)

        n_w = 3 * PARTS * 2
        h1, h3, h2 = pl.pallas_call(
            functools.partial(weights_kernel, side, loc),
            out_shape=[jax.ShapeDtypeStruct(w.shape[1:], BF16) for w in (w1, w3, w2)],
            in_specs=[ANY] * 3,
            out_specs=[ANY] * 3,
            scratch_shapes=[pltpu.SemaphoreType.DMA((n_w,))] * 4,
            compiler_params=pltpu.CompilerParams(collective_id=0, has_side_effects=True),
            name="weights",
        )(w1, w3, w2)

        dma = pltpu.SemaphoreType.DMA
        recvl, recvr = pl.pallas_call(
            functools.partial(dispatch_kernel, side, cap),
            out_shape=[jax.ShapeDtypeStruct((side, side, 2, cap, c), BF16) for c in (cl, cr)],
            in_specs=[ANY] * 3,
            out_specs=[ANY] * 2,
            scratch_shapes=[
                pltpu.VMEM((side, td, cl), BF16),
                pltpu.VMEM((side, td, cr), BF16),
                pltpu.VMEM((side, side, 2 * loc, td), F32),
                pltpu.VMEM((side, side, 2 * loc, td), F32),
                pltpu.VMEM((2 * cap, td), BF16),
                pltpu.VMEM((side, side, 2, cap, cl), BF16),
                pltpu.VMEM((side, side, 2, cap, cr), BF16),
                dma((2, 2)),
                dma((2, 4)),
                dma((2, 4)),
                dma((2, 4)),
                dma((2, 4)),
                dma((side, side, 2)),
                dma((side, side, 2)),
                dma((side, side, 2)),
                dma((side, side, 2)),
            ],
            compiler_params=pltpu.CompilerParams(collective_id=1, has_side_effects=True, vmem_limit_bytes=60 << 20),
            name="dispatch",
        )(x, ml, mr)

        steps = side * side
        blocks = [jax.ShapeDtypeStruct((steps, 2, cap, c), BF16) for c in (cl, cr)]
        y = pl.pallas_call(
            functools.partial(experts_kernel, side, cap, loc),
            out_shape=[jax.ShapeDtypeStruct((td, d), BF16)] + blocks + blocks,
            in_specs=[SMEM] + [ANY] * 9 + [VMEM] * 3,
            out_specs=[VMEM] + [ANY] * 4,
            scratch_shapes=[
                pltpu.VMEM((2, d, ff), BF16),
                pltpu.VMEM((2, d, ff), BF16),
                pltpu.VMEM((2, ff, d), BF16),
                pltpu.VMEM((2, 2, cap, cl), BF16),
                pltpu.VMEM((2, 2, cap, cr), BF16),
                pltpu.VMEM((2, 2 * cap, d), BF16),
                pltpu.VMEM((2, 2 * cap, ff), BF16),
                pltpu.VMEM((RING, 2, cap, cl), BF16),
                pltpu.VMEM((RING, 2, cap, cr), BF16),
                pltpu.VMEM((2, cap, cl), BF16),
                pltpu.VMEM((2, cap, cr), BF16),
                pltpu.VMEM((2 * cap, td), BF16),
                pltpu.VMEM((td, d), F32),
                dma((3,)),
                dma((2, 2)),
                dma((2,)),
                dma((2,)),
                dma((steps, 2)),
                dma((steps, 2)),
                dma((steps,)),
                dma((steps,)),
                dma((steps, 2)),
                dma((steps, 2)),
                dma((steps, 2)),
                dma((steps, 2)),
            ],
            compiler_params=pltpu.CompilerParams(collective_id=2, has_side_effects=True, vmem_limit_bytes=63 << 20),
            name="experts",
        )(n0, x, recvl, recvr, w1, w3, w2, h1, h3, h2, pc.reshape(steps, 2 * loc, td), gc, gt[0].reshape(td, 1))[0]
        return y

    spec_t = P(("dp", "ep"), None)
    spec_w = P("ep", None, None)
    return jax.shard_map(local, mesh=mesh, in_specs=(spec_t, spec_t, spec_t, spec_w, spec_w, spec_w), out_specs=spec_t, check_vma=False)
```

time: 2240 us -> 753 us (0.34); the launches traced: 2210 us -> 753 us
  local copies, waits for them, and re-layouts: 719 us -> 7.36 us
  Pallas kernels: 120 us -> 732 us
  starting transfers between devices: 516 us -> 8.31 us
  other arithmetic: 365 us -> 4.74 us
  waiting for transfers between devices: 359 us -> 0.01 us
  matrix products: 63 us -> 0.44 us
  blocking collectives: 44.9 us -> 0 us
    pallas_call x0 -> x3, Pallas kernels: none -> 732 us  [the longest x1 403 us: local(): pl.pallas_call(functools.partial(experts_kernel, side, cap, loc), out_sha...]
    gather x4 -> x0, local copies, waits for them, and re-layouts: 584 us -> none  [the longest x1 287 us: grouped_ffn(): xs = rows[perm]]
    ppermute x62 -> x0, starting transfers between devices: 410 us -> none  [the longest x31 386 us: local(): hblocks.append(lax.ppermute(blk, 'ep', pairs))]
    ppermute x62 -> x0, waiting for transfers between devices: 359 us -> none  [the longest x31 352 us: local(): back.append(lax.ppermute(hout[dl], 'ep', pairs))]
    reduce_sum x7 -> x2, other arithmetic: 190 us -> 1.11 us  [the longest x1 0.92 us: plan(): g = jnp.sum(jnp.where(hit, gates.astype(F32)[:, :, None], 0.0), axis=1)]
    another operation x3 -> x0, Pallas kernels: 118 us -> none
    all_to_all x3 -> x1, starting transfers between devices: 106 us -> 8.31 us  [local(): n0 = lax.all_to_all(n0.reshape(p, 1), 'ep', 0, 0, tiled=True).reshape(p)]
    convert_element_type x4 -> x2, other arithmetic: 88.8 us -> 1.32 us  [the longest x1 0.71 us: plan(): g = jnp.sum(jnp.where(hit, gates.astype(F32)[:, :, None], 0.0), axis=1)]
  transfers between devices with their start and end apart: 65 -> 1, of which waited for: 5 -> 0; matrix products, arithmetic and copies ran while one was open for 15% -> 1% of each run, Pallas kernels for 0% -> 44%
where the time goes in v1:
time: 753 us
  Pallas kernels  732 us (97%)
  starting transfers between devices  8.31 us (1%)
    pallas_call x1, Pallas kernels, local(): pl.pallas_call(functools.partial(experts_kernel, side, cap, loc), out_sha...  403 us
    pallas_call x1, Pallas kernels, local(): pl.pallas_call(functools.partial(dispatch_kernel, side, cap), out_shape=[...  223 us
    pallas_call x1, Pallas kernels, local(): pl.pallas_call(functools.partial(weights_kernel, side, loc), out_shape=[j...  106 us
  transfers between devices with their start and end apart: 1, of which 0 were waited for; matrix products, arithmetic and copies ran while one was open for 1% of the time, Pallas kernels for 44%

profile of v1, /device:TPU:99, one launch (start us, length us, event | category | flops | bytes accessed | tf_op | source)
XLA Modules:
  0.0 752.6 jit_solution(7820186855906597317)
XLA Ops:
  0.0 0.9 fusion.1
  0.9 0.2 convert_reduce_fusion
  1.1 0.1 reshape.32
  1.2 0.6 slice_convert_fusion
  1.9 8.3 %all-to-all-start = ((s32[32,1,1]{2,1,0:T(1,128)}), s32[32,1,1]{2,1,0:T(1,128)S(1)}, u32[]{:S(2)}, u32[]{:S(2)}) async-start(s32[32,1,1]{2,1,0:T(1,128)} %bitcast), calls=%async_computation | async-start | bytes 32768 | tf_op jit(solution)/shard_map/all_to_all | solution.py:554
  10.2 0.7 convert_element_type.14
  10.9 0.9 select_reduce_fusion
  11.8 0.7 reshape.35.gt
  12.6 0.2 reduce_window_sum.13
  12.7 0.1 reduce_window_sum.14
  12.8 0.4 fusion.3
  13.3 0.1 reshape.34.ml
  13.4 0.0 copy-start
  13.4 0.7 reshape_reshape.3.pt
  14.1 0.7 copy.28
  14.8 0.9 copy.26.gh
  15.7 0.0 copy-done
  15.7 222.6 %dispatch.1 = (bf16[4,4,2,192,768]{4,3,2,1,0:T(8,128)(2,1)}, bf16[4,4,2,192,1280]{4,3,2,1,0:T(8,128)(2,1)}) custom-call(bf16[768,2048]{1,0:T(8,128)(2,1)} %x.3, f32[4,4,4,768]{3,2,1,0:T(4,128)} %copy-done, f32[4,4,4,768]{3,2,1,0:T(4,128)} %bitcast.11), custom_call_target="tpu_custom_call" | custom-call | tf_op jit(solution)/shard_map/dispatch/pallas_call | solution.py:571
  238.3 106.0 %weights.1 = (bf16[2048,1024]{1,0:T(8,128)(2,1)}, bf16[2048,1024]{1,0:T(8,128)(2,1)}, bf16[1024,2048]{1,0:T(8,128)(2,1)}) custom-call(bf16[3,2048,1024]{2,1,0:T(8,128)(2,1)} %w1.3, bf16[3,2048,1024]{2,1,0:T(8,128)(2,1)} %w3.3, bf16[3,1024,2048]{2,1,0:T(8,128)(2,1)} %w2.3), custom_call_target="tpu_custom_call" | custom-call | tf_op jit(solution)/shard_map/weights/pallas_call | solution.py:560
  344.3 0.0 all-to-all-done
  344.3 1.2 reduce.n0
  345.5 403.1 %experts.1 = (bf16[768,2048]{1,0:T(8,128)(2,1)}, bf16[16,2,192,768]{3,2,1,0:T(8,128)(2,1)}, bf16[16,2,192,1280]{3,2,1,0:T(8,128)(2,1)}, bf16[16,2,192,768]{3,2,1,0:T(8,128)(2,1)}, bf16[16,2,192,1280]{3,2,1,0:T(8,128)(2,1)}) custom-call(s32[32]{0:T(128)} %reduce.n0, bf16[768,2048]{1,0:T(8,128)(2,1)} %x.3, ...), custom_call_target="tpu_custom_call" | custom-call | tf_op jit(solution)/shard_map/experts/pallas_call | solution.py:600
  748.6 4.0 copy.30
  (3 shorter events, 0.0 us)
Async XLA Ops:
  1.9 342.4 %all-to-all-start = ((s32[32,1,1]{2,1,0:T(1,128)}), s32[32,1,1]{2,1,0:T(1,128)S(1)}, u32[]{:S(2)}, u32[]{:S(2)}) async-start(s32[32,1,1]{2,1,0:T(1,128)} %bitcast), calls=%async_computation | async-start | bytes 32768 | tf_op jit(solution)/shard_map/all_to_all | solution.py:554
  13.4 2.4 copy-start

commit v2 on v1

v2 whole, which is shorter than its diff:
```python
import functools
import math

import jax
import jax.numpy as jnp
from jax import lax
from jax.experimental import pallas as pl
from jax.experimental.pallas import tpu as pltpu
from jax.sharding import PartitionSpec as P

MESH = pl.DeviceIdType.MESH
ANY = pl.BlockSpec(memory_space=pl.ANY)
SMEM = pl.BlockSpec(memory_space=pltpu.SMEM)
VMEM = pl.BlockSpec(memory_space=pltpu.VMEM)
F32 = jnp.float32
BF16 = jnp.bfloat16
NT = 256
CT = 512
WT = 512
RING = 6
LAG_F = 3
LAG_C = 8
PARTS = 2


def holder_list(p):
    return [0, (p // 2 + 1) % p, (p // 4 + 2) % p, (3 * p // 4 + 3) % p]


class Place:
    def __init__(self, side):
        me = lax.axis_index("ep")
        self.side = side
        self.z = lax.axis_index("dp")
        self.c = lax.rem(me, 2)
        self.x = lax.rem(lax.div(me, 2), side)
        self.y = lax.div(me, 2 * side)

    def index(self, dy, dx, c):
        s = self.side
        return (lax.rem(self.y + dy, s) * s + lax.rem(self.x + dx, s)) * 2 + c

    def dev(self, dy, dx, c):
        return (self.z, self.index(dy, dx, c))

    def greet(self):
        bar = pltpu.get_barrier_semaphore()
        near = [self.dev(0, 0, 1 - self.c)]
        for k in range(1, self.side):
            for c in range(2):
                near += [self.dev(0, k, c), self.dev(k, 0, c)]
        for d in near:
            pl.semaphore_signal(bar, inc=1, device_id=d, device_id_type=MESH)
        pl.semaphore_wait(bar, len(near))


def remote(src, dst, ssem, rsem, dev):
    return pltpu.make_async_remote_copy(src_ref=src, dst_ref=dst, send_sem=ssem, recv_sem=rsem, device_id=dev, device_id_type=MESH)


def keep(src, dst, sem):
    return pltpu.make_async_copy(src, dst, sem)


class Chain:
    def __init__(self, at, loc, pairs, s_sem, r_sem, p_sem, q_sem):
        side = self.side = at.side
        hx, hc = lax.rem(at.y, 2), lax.div(at.y, 2)
        self.slot = lax.div(at.y + side - 1, side) * loc
        self.rel = lax.rem(at.x + side - hx, side)
        self.lane = at.c == hc
        self.next = (at.dev(0, 1, at.c), at.dev(0, side - 1, at.c))
        self.mate = at.dev(0, 0, 1 - at.c)
        self.sems = s_sem, r_sem, p_sem, q_sem
        self.pieces = []
        for m, (w, h) in enumerate(pairs):
            n = w.shape[1] // (2 * PARTS)
            for i in range(PARTS):
                j = (m * PARTS + i) * 2
                self.pieces.append([(w, h, pl.ds((half * PARTS + i) * n, n), j + half) for half in range(2)])
        self.slots = len(self.pieces) + side - 1

    def hop(self, src, dst, j, half):
        return remote(src, dst, self.sems[0].at[j], self.sems[1].at[j], self.next[half])

    def pass_on(self, src, dst, j):
        return remote(src, dst, self.sems[2].at[j], self.sems[3].at[j], self.mate)

    def begin(self):
        @pl.when(jnp.logical_and(self.lane, self.rel == 0))
        def _():
            for pair in self.pieces:
                for half, (w, h, rows, j) in enumerate(pair):
                    self.hop(w.at[self.slot, rows], h.at[rows], j, half).start()
            for pair in self.pieces:
                for w, h, rows, j in pair:
                    self.pass_on(w.at[self.slot, rows], h.at[rows], j).start()

    def due(self, r, n):
        for half in range(2):
            i = n - (r if half == 0 else self.side - r)
            if 0 <= i < len(self.pieces):
                w, h, rows, j = self.pieces[i][half]
                yield half, h.at[rows], j, (r < self.side - 1) if half == 0 else (r > 1)

    def serve(self, n):
        def relay(r):
            for half, part, j, more in self.due(r, n):
                self.hop(part, part, j, half).wait_recv()
                if more:
                    self.hop(part, part, j, half).start()
                self.pass_on(part, part, j).start()

        for r in range(1, self.side):
            pl.when(jnp.logical_and(self.lane, self.rel == r))(functools.partial(relay, r))

    def finish(self):
        @pl.when(jnp.logical_and(self.lane, self.rel == 0))
        def _():
            for pair in self.pieces:
                for half, (w, h, rows, j) in enumerate(pair):
                    self.hop(w.at[self.slot, rows], h.at[rows], j, half).wait_send()
                    self.pass_on(w.at[self.slot, rows], h.at[rows], j).wait_send()

        def relay(r):
            for n in range(self.slots + 1):
                for half, part, j, more in self.due(r, n):
                    self.pass_on(part, part, j).wait_send()
                    if more:
                        self.hop(part, part, j, half).wait_send()

        for r in range(1, self.side):
            pl.when(jnp.logical_and(self.lane, self.rel == r))(functools.partial(relay, r))

        @pl.when(jnp.logical_not(self.lane))
        def _():
            for pair in self.pieces:
                for w, h, rows, j in pair:
                    self.pass_on(h.at[rows], h.at[rows], j).wait_recv()


def dispatch_kernel(
    side, cap, loc, x, ml, mr, w1, w3, w2, recvl, recvr, h1, h3, h2,
    xl, xr, mlv, mrv, sel, sbl, sbr, own, ag_s, ag_r, m_s, m_r, s_l, r_l, s_r, r_r, *w_sems,
):
    at = Place(side)
    chain = Chain(at, loc, ((w1, h1), (w3, h3), (w2, h2)), *w_sems)
    td = x.shape[0]
    cl, cr = xl.shape[2], xr.shape[2]
    half = td // 2
    sides = (
        dict(i=0, xv=xl, cols=pl.ds(0, cl), m=ml, mv=mlv, sb=sbl, rv=recvl, ss=s_l, rs=r_l, axis=0),
        dict(i=1, xv=xr, cols=pl.ds(cl, cr), m=mr, mv=mrv, sb=sbr, rv=recvr, ss=s_r, rs=r_r, axis=1),
    )

    def along(a, k, c):
        return at.dev(k, 0, c) if a == 0 else at.dev(0, k, c)

    mine = []
    for t in sides:
        i, here = t["i"], at.y if t["axis"] == 0 else at.x
        mine.append(pltpu.make_async_copy(x.at[:, t["cols"]], t["xv"].at[0], own.at[i, 0]))
        mine.append(pltpu.make_async_copy(t["m"].at[here], t["mv"].at[0], own.at[i, 1]))
    for cp in mine:
        cp.start()
    at.greet()
    last = side - 1
    sends = []
    for t in sides:
        i, a, here = t["i"], t["axis"], at.y if t["axis"] == 0 else at.x
        for k in range(1, side):
            sends.append(remote(t["m"].at[lax.rem(here + k, side)], t["mv"].at[side - k], m_s.at[i, k], m_r.at[i, side - k], along(a, k, at.c)))
        sends.append(remote(x.at[:, t["cols"]], t["xv"].at[last], ag_s.at[i, 0], ag_r.at[i, last], along(a, 1, at.c)))
        sends.append(remote(x.at[:, t["cols"]], t["xv"].at[1], ag_s.at[i, 1], ag_r.at[i, 1], along(a, last, at.c)))
    for cp in sends:
        cp.start()
    chain.begin()

    def pack(t, k):
        there = at.x if t["axis"] == 0 else at.y
        width = t["xv"].shape[2]

        def one(d, carry):
            q = lax.rem(there + d, side)
            r = lax.broadcasted_iota(jnp.int32, (cap, td), 0).astype(F32)
            for c in range(2):
                p0 = t["mv"][k, q, 2 * c : 2 * c + 1, :]
                p1 = t["mv"][k, q, 2 * c + 1 : 2 * c + 2, :]
                hit = jnp.logical_or(r == p0, r == p1)
                sel[c * cap : (c + 1) * cap, :] = jnp.where(hit, 1.0, 0.0).astype(BF16)

            def col(n, carry):
                cols = pl.ds(pl.multiple_of(n * WT, WT), WT)
                o = jnp.dot(sel[...], t["xv"][k, :, cols], preferred_element_type=F32).astype(BF16)
                t["sb"][k, d, :, :, cols] = o.reshape(2, cap, WT)
                return carry

            return lax.fori_loop(0, width // WT, col, carry)

        lax.fori_loop(0, side, one, 0)

    def block(t, k, d, c):
        to = (side - d) % side
        slot = (k, to, at.c) if t["axis"] == 0 else (to, k, at.c)
        return remote(t["sb"].at[k, d, c], t["rv"].at[slot], t["ss"].at[k, d, c], t["rs"].at[slot], along(1 - t["axis"], d, c))

    def send(t, k):
        for d in (1, side - 1, 2):
            for c in range(2):
                block(t, k, d, c).start()
        block(t, k, 0, 1 - at.c).start()
        slot = (k, 0, at.c) if t["axis"] == 0 else (0, k, at.c)
        pltpu.make_async_copy(t["sb"].at[k, 0, at.c], t["rv"].at[slot], t["rs"].at[slot]).start()

    lside, rside = sides
    fwd = {}

    def pass_along(t):
        i, a, xv = t["i"], t["axis"], t["xv"]
        fwd[i] = []
        for k, rows, to in ((last, pl.ds(0, half), 1), (1, pl.ds(half, half), last)):
            remote(xv.at[k], xv.at[k], ag_s.at[i, 0], ag_r.at[i, k], along(a, 1, at.c)).wait_recv()
            cp = remote(xv.at[k, rows], xv.at[2, rows], ag_s.at[i, 2 if to == 1 else 3], ag_r.at[i, 2 if to == 1 else 0], along(a, to, at.c))
            cp.start()
            fwd[i].append(cp)
        for k in range(1, side):
            remote(t["mv"].at[k], t["mv"].at[k], m_s.at[i, k], m_r.at[i, k], along(a, 1, at.c)).wait_recv()

    for cp in mine:
        cp.wait()
    pack(rside, 0)
    pack(lside, 0)
    send(rside, 0)
    pass_along(lside)
    pack(lside, last)
    pass_along(rside)
    pack(rside, last)
    pack(lside, 1)
    send(rside, last)
    pack(rside, 1)
    chain.serve(1)
    send(rside, 1)
    send(lside, 0)
    for cp in fwd[0]:
        cp.wait_recv()
    pack(lside, 2)
    chain.serve(2)
    send(lside, last)
    chain.serve(3)
    for cp in fwd[1]:
        cp.wait_recv()
    pack(rside, 2)
    chain.serve(4)
    send(rside, 2)
    send(lside, 1)
    chain.serve(5)
    chain.serve(6)
    send(lside, 2)
    for n in range(7, chain.slots + 1):
        chain.serve(n)
    for cp in sends + fwd[0] + fwd[1]:
        cp.wait_send()

    def settle(j, carry):
        k, d, c = lax.div(j, 2 * side), lax.rem(lax.div(j, 2), side), lax.rem(j, 2)
        for t in sides:
            dst = t["rv"].at[k, d, c]
            remote(t["sb"].at[0, 0, 0], dst, t["ss"].at[k, d, c], t["rs"].at[k, d, c], along(0, 1, at.c)).wait_recv()

            @pl.when(jnp.logical_or(d != 0, c != at.c))
            def _():
                remote(t["sb"].at[k, d, c], dst, t["ss"].at[k, d, c], t["rs"].at[k, d, c], along(0, 1, at.c)).wait_send()

        return carry

    lax.fori_loop(0, 2 * side * side, settle, 0)
    chain.finish()


def experts_kernel(
    side, cap, slot_last, n0, x, recvl, recvr, w1, w3, w2, h1, h3, h2, pt, gt, gh,
    y, rell, relr, retl, retr,
    w1v, w3v, w2v, xbl, xbr, xs, av, ol, orr, ocl, ocr, gm, yacc,
    w_sem, u_sem, x_sem, c_sem, s1l, s1r, r1l, r1r, s2l, s2r, r2l, r2r,
):
    at = Place(side)
    td = x.shape[0]
    cl, cr = ol.shape[3], orr.shape[3]
    d_model, ff = w1.shape[1], w1.shape[2]
    steps = side * side
    n_rel = (side - 1) * (side - 1)
    m2 = 2 * cap

    def where_to(s):
        b = lax.div(s, n_rel)
        t = s - b * n_rel
        r, q = lax.rem(t, 3), lax.div(t, 3)
        e, f = lax.rem(t, 2), lax.div(t, 2)
        dx = (1 - b) * (1 + r) + b * (1 - e) * (1 + f)
        dy = (1 - b) * (1 + lax.rem(r + q, 3)) + b * e * (1 + f)
        return lax.rem(dy, side), lax.rem(dx, side)

    def load_w(w, v, i):
        return pltpu.make_async_copy(w, v, w_sem.at[i])

    def load_up(f):
        cols = pl.ds(pl.multiple_of(f * NT, NT), NT)
        return [pltpu.make_async_copy(w.at[pl.ds(0, 2), :, cols], v.at[:, :, cols], u_sem.at[i, f]) for i, (w, v) in enumerate(((w1, w1v), (w3, w3v)))]

    def ends(s):
        dy, dx = where_to(s)
        return (dy, dx), (lax.rem(side - dy, side), lax.rem(side - dx, side))

    def load_x(s):
        slot = lax.rem(s, 2)
        return [
            pltpu.make_async_copy(r.at[dy, dx, j], xb.at[slot, j], x_sem.at[slot, 2 * h + j])
            for j, (dy, dx) in enumerate(ends(s))
            for h, (r, xb) in enumerate(((recvl, xbl), (recvr, xbr)))
        ]

    for cp in load_x(0):
        cp.start()
    for f in range(ff // NT):
        for cp in load_up(f):
            cp.start()
    load_w(w2.at[pl.ds(0, 2)], w2v, 0).start()
    yacc[...] = jnp.zeros_like(yacc)
    at.greet()

    halves = ((ol, rell, retl, s1l, r1l, s2l, r2l), (orr, relr, retr, s1r, r1r, s2r, r2r))

    def first_hop(s, h):
        o, rel, ret, s1, r1, s2, r2 = halves[h]
        so = lax.rem(s, RING)
        relay, direct = [], []
        for j, (dy, dx) in enumerate(ends(s)):
            via = at.dev(0, dx, at.c) if h == 0 else at.dev(dy, 0, at.c)
            relay.append(remote(o.at[so, j], rel.at[s, j], s1.at[s, j], r1.at[s, j], via))
            direct.append(remote(o.at[so, j], ret.at[s, at.c], s1.at[s, j], r2.at[s, at.c], at.dev(dy, dx, j)))
        mate = remote(o.at[so, 1 - at.c], ret.at[s, at.c], s1.at[s, 0], r2.at[s, at.c], at.dev(0, 0, 1 - at.c))
        self_cp = keep(o.at[so, at.c], ret.at[s, at.c], r2.at[s, at.c])
        return relay, direct, mate, self_cp

    def start_first(s):
        hops = [first_hop(s, h) for h in range(2)]

        @pl.when(s < n_rel)
        def _():
            for relay, *_ in hops:
                for cp in relay:
                    cp.start()

        @pl.when(jnp.logical_and(s >= n_rel, s < steps - 1))
        def _():
            for _, direct, *_ in hops:
                for cp in direct:
                    cp.start()

        @pl.when(s == steps - 1)
        def _():
            for *_, mate, self_cp in hops:
                mate.start()
                self_cp.start()

    def wait_first(s):
        hops = [first_hop(s, h) for h in range(2)]

        @pl.when(s < steps - 1)
        def _():
            for _, direct, *_ in hops:
                for cp in direct:
                    cp.wait_send()

        @pl.when(s == steps - 1)
        def _():
            for *_, mate, _ in hops:
                mate.wait_send()

    def second_hop(s, h):
        o, rel, ret, s1, r1, s2, r2 = halves[h]
        got, on = [], []
        for j, (dy, dx) in enumerate(ends(s)):
            got.append(remote(rel.at[s, j], rel.at[s, j], s1.at[s, j], r1.at[s, j], at.dev(0, 1, at.c)))
            to = at.dev(dy, 0, j) if h == 0 else at.dev(0, dx, j)
            on.append(remote(rel.at[s, j], ret.at[s, at.c], s2.at[s, j], r2.at[s, at.c], to))
        return got, on

    def forward(s):
        for h in range(2):
            for cp, on in zip(*second_hop(s, h)):
                cp.wait_recv()
                on.start()

    def fetch(p):
        for i in range(2):
            s = 2 * p + i
            for h, oc in enumerate((ocl, ocr)):
                o, rel, ret, s1, r1, s2, r2 = halves[h]
                for c in range(2):
                    remote(ret.at[s, c], ret.at[s, c], s2.at[s, c], r2.at[s, c], at.dev(0, 1, at.c)).wait_recv()
                pltpu.make_async_copy(ret.at[s], oc.at[i], c_sem.at[h, i]).start()

    def combine(p):
        for i in range(2):
            dy, dx = where_to(2 * p + i)
            oy = at.c * dy + (1 - at.c) * (side - dy)
            ox = at.c * dx + (1 - at.c) * (side - dx)
            chip = lax.rem(at.y + oy, side) * side + lax.rem(at.x + ox, side)
            r = lax.broadcasted_iota(jnp.int32, (cap, td), 0).astype(F32)
            for c in range(2):
                g = jnp.zeros((cap, td), F32)
                for j in range(2):
                    row = 2 * c + j
                    g = g + jnp.where(r == pt[chip, row : row + 1, :], gt[chip, row : row + 1, :], 0.0)
                lo = (2 * i + c) * cap
                gm[lo : lo + cap, :] = g.astype(BF16)
        for h, oc in enumerate((ocl, ocr)):
            for i in range(2):
                pltpu.make_async_copy(halves[h][2].at[2 * p + i], oc.at[i], c_sem.at[h, i]).wait()
            width = cl if h == 0 else cr

            def col(n, carry):
                cols = pl.ds(pl.multiple_of(n * CT, CT), CT)
                to = pl.ds(pl.multiple_of(h * cl + n * CT, CT), CT)
                b = oc[:, :, :, cols].reshape(2 * m2, CT)
                yacc[:, to] += lax.dot_general(gm[...], b, (((0,), (0,)), ((), ())), preferred_element_type=F32)
                return carry

            lax.fori_loop(0, width // CT, col, 0)

    def step(s, carry):
        slot, so = lax.rem(s, 2), lax.rem(s, RING)

        @pl.when(s + 1 < steps)
        def _():
            for cp in load_x(s + 1):
                cp.start()

        for cp in load_x(s):
            cp.wait()
        cuts = [n0[at.index(dy, dx, j)] for j, (dy, dx) in enumerate(ends(s))]
        for c in range(2):
            for xb, lo, width in ((xbl, 0, cl), (xbr, cl, cr)):
                for n in range(width // NT):
                    v = xb[slot, c, :, n * NT : (n + 1) * NT].astype(F32)
                    first = lax.broadcasted_iota(jnp.int32, (cap, NT), 0) < cuts[c]
                    z = jnp.zeros_like(v)
                    to = slice(lo + n * NT, lo + (n + 1) * NT)
                    xs[0, c * cap : (c + 1) * cap, to] = jnp.where(first, v, z).astype(BF16)
                    xs[1, c * cap : (c + 1) * cap, to] = jnp.where(first, z, v).astype(BF16)

        def up2(f, carry):
            @pl.when(s == 0)
            def _():
                for cp in load_up(f):
                    cp.wait()

            cols = pl.ds(pl.multiple_of(f * NT, NT), NT)
            u = sum(jnp.dot(xs[e], w1v[e, :, cols], preferred_element_type=F32) for e in range(2))
            v = sum(jnp.dot(xs[e], w3v[e, :, cols], preferred_element_type=F32) for e in range(2))
            a = (jax.nn.silu(u) * v).astype(BF16).astype(F32)
            row = lax.broadcasted_iota(jnp.int32, (cap, NT), 0)
            first = jnp.concatenate([jnp.where(row < cuts[c], 1.0, 0.0) for c in range(2)], axis=0)
            a0 = jnp.where(first > 0.5, a, 0.0)
            av[0, :, cols] = a0.astype(BF16)
            av[1, :, cols] = (a - a0).astype(BF16)
            return carry

        lax.fori_loop(0, ff // NT, up2, 0)

        @pl.when(s == 0)
        def _():
            load_w(w2.at[pl.ds(0, 2)], w2v, 0).wait()

        @pl.when(s >= RING)
        def _():
            wait_first(s - RING)

        for o, lo, width in ((ol, 0, cl), (orr, cl, cr)):

            def down(n, carry):
                to = pl.ds(pl.multiple_of(n * WT, WT), WT)
                cols = pl.ds(pl.multiple_of(lo + n * WT, WT), WT)
                r = sum(jnp.dot(av[e], w2v[e, :, cols], preferred_element_type=F32) for e in range(2))
                o[so, :, :, to] = r.astype(BF16).reshape(2, cap, WT)
                return carry

            lax.fori_loop(0, width // WT, down, 0)

        @pl.when(jnp.logical_and(s >= LAG_F, s - LAG_F < n_rel))
        def _():
            forward(s - LAG_F)

        start_first(s)
        late = s - LAG_C
        odd = lax.rem(late + 2 * steps, 2)

        @pl.when(jnp.logical_and(late >= 0, odd == 0))
        def _():
            fetch(lax.div(late, 2))

        @pl.when(jnp.logical_and(late >= 0, odd == 1))
        def _():
            combine(lax.div(late, 2))

        return carry

    lax.fori_loop(0, steps, step, 0)

    is_h = jnp.logical_and(at.x == lax.rem(at.y, 2), at.c == lax.div(at.y, 2))
    hs = lax.div(at.y + side - 1, side) * slot_last
    for i, (w, h, v) in enumerate(((w1, h1, w1v), (w3, h3, w3v), (w2, h2, w2v))):

        @pl.when(is_h)
        def _():
            load_w(w.at[hs], v.at[0], i).start()

        @pl.when(jnp.logical_not(is_h))
        def _():
            load_w(h, v.at[0], i).start()

    def load_own(i):
        return pltpu.make_async_copy(x.at[pl.ds(i * m2, m2)], xs.at[i], x_sem.at[i, 0])

    for i in range(td // m2):
        load_own(i).start()

    begun = (steps - LAG_C) // 2
    if (steps - LAG_C) % 2:
        raise ValueError("odd lag")

    def drain(p, carry):
        fetch(p)
        combine(p)
        return carry

    lax.fori_loop(begun, steps // 2 - 2, drain, 0)
    fetch(steps // 2 - 2)
    for i, (h, v) in enumerate(((h1, w1v), (h3, w3v), (h2, w2v))):
        load_w(h, v.at[0], i).wait()
    for i in range(td // m2):
        load_own(i).wait()

        def up1(f, carry):
            cols = pl.ds(pl.multiple_of(f * NT, NT), NT)
            u = jnp.dot(xs[i], w1v[0, :, cols], preferred_element_type=F32)
            v = jnp.dot(xs[i], w3v[0, :, cols], preferred_element_type=F32)
            av[0, :, cols] = (jax.nn.silu(u) * v).astype(BF16)
            return carry

        lax.fori_loop(0, ff // NT, up1, 0)

        def down1(n, carry):
            cols = pl.ds(pl.multiple_of(n * WT, WT), WT)
            r = jnp.dot(av[0], w2v[0, :, cols], preferred_element_type=F32).astype(BF16).astype(F32)
            g = gh[i * m2 : (i + 1) * m2, :]
            yacc[i * m2 : (i + 1) * m2, cols] += jnp.where(g > 0.0, g * r, 0.0)
            return carry

        lax.fori_loop(0, d_model // WT, down1, 0)

    combine(steps // 2 - 2)
    drain(steps // 2 - 1, 0)

    def out(n, carry):
        cols = pl.ds(pl.multiple_of(n * NT, NT), NT)
        for i in range(td // m2):
            xs[i, :, cols] = yacc[i * m2 : (i + 1) * m2, cols].astype(BF16)
        return carry

    lax.fori_loop(0, d_model // NT, out, 0)
    done = [pltpu.make_async_copy(xs.at[i], y.at[pl.ds(i * m2, m2)], x_sem.at[i, 0]) for i in range(td // m2)]
    for cp in done:
        cp.start()

    def settle(s, carry):
        wait_first(s)
        return carry

    lax.fori_loop(steps - RING, steps, settle, 0)

    def settle2(s, carry):
        for h in range(2):
            for cp in second_hop(s, h)[1]:
                cp.wait_send()
        return carry

    lax.fori_loop(0, n_rel, settle2, 0)
    for cp in done:
        cp.wait()


def plan(ridx, gates, p, experts):
    td, k = ridx.shape
    ids = jnp.arange(experts, dtype=ridx.dtype)
    hit = ridx[:, :, None] == ids
    g = jnp.sum(jnp.where(hit, gates.astype(F32)[:, :, None], 0.0), axis=1)
    m = jnp.logical_and(jnp.any(hit, axis=1), ids[None, :] > 0)
    mb = m.astype(BF16)
    tri = (jnp.arange(td)[:, None] > jnp.arange(td)[None, :]).astype(BF16)
    rank = jnp.dot(tri, mb, preferred_element_type=F32)
    cnt = jnp.sum(m.astype(F32), axis=0)
    loc = experts // p
    before = jnp.cumsum(cnt.reshape(p, loc), axis=1) - cnt.reshape(p, loc)
    pos = jnp.where(m, rank + before.reshape(-1), -1.0)
    return pos.T, g.T, cnt.reshape(p, loc)[:, 0].astype(jnp.int32)


def solution(mesh):
    p = mesh.shape["ep"]
    side = math.isqrt(p // 2)
    want = [(y * side + y % 2) * 2 + y // 2 for y in range(side)]
    if side != 4 or sorted(holder_list(p)) != sorted(want) or holder_list(p)[0] != want[0]:
        raise ValueError("unknown placement")

    def local(x, ridx, gates, w1, w3, w2):
        td, d = x.shape
        k = ridx.shape[1]
        slots, _, ff = w1.shape
        loc = slots - 1
        cap = td * k // p
        cl = d // 4
        cr = d - cl
        pt, gt, n0 = plan(ridx, gates, p, p * loc)
        n0 = lax.all_to_all(n0.reshape(p, 1), "ep", 0, 0, tiled=True).reshape(p)
        pc = pt.reshape(side, side, 2 * loc, td)
        ml, mr = pc, pc.transpose(1, 0, 2, 3)
        gc = gt.reshape(side * side, 2 * loc, td)

        dma = pltpu.SemaphoreType.DMA
        recvl, recvr, h1, h3, h2 = pl.pallas_call(
            functools.partial(dispatch_kernel, side, cap, loc),
            out_shape=[jax.ShapeDtypeStruct((side, side, 2, cap, c), BF16) for c in (cl, cr)]
            + [jax.ShapeDtypeStruct(w.shape[1:], BF16) for w in (w1, w3, w2)],
            in_specs=[ANY] * 6,
            out_specs=[ANY] * 5,
            scratch_shapes=[
                pltpu.VMEM((side, td, cl), BF16),
                pltpu.VMEM((side, td, cr), BF16),
                pltpu.VMEM((side, side, 2 * loc, td), F32),
                pltpu.VMEM((side, side, 2 * loc, td), F32),
                pltpu.VMEM((2 * cap, td), BF16),
                pltpu.VMEM((side, side, 2, cap, cl), BF16),
                pltpu.VMEM((side, side, 2, cap, cr), BF16),
                dma((2, 2)),
                dma((2, 4)),
                dma((2, 4)),
                dma((2, 4)),
                dma((2, 4)),
                dma((side, side, 2)),
                dma((side, side, 2)),
                dma((side, side, 2)),
                dma((side, side, 2)),
            ]
            + [dma((6 * PARTS,))] * 4,
            compiler_params=pltpu.CompilerParams(collective_id=0, has_side_effects=True, vmem_limit_bytes=60 << 20),
            name="dispatch",
        )(x, ml, mr, w1, w3, w2)

        steps = side * side
        blocks = [jax.ShapeDtypeStruct((steps, 2, cap, c), BF16) for c in (cl, cr)]
        y = pl.pallas_call(
            functools.partial(experts_kernel, side, cap, loc),
            out_shape=[jax.ShapeDtypeStruct((td, d), BF16)] + blocks + blocks,
            in_specs=[SMEM] + [ANY] * 9 + [VMEM] * 3,
            out_specs=[ANY] * 5,
            scratch_shapes=[
                pltpu.VMEM((2, d, ff), BF16),
                pltpu.VMEM((2, d, ff), BF16),
                pltpu.VMEM((2, ff, d), BF16),
                pltpu.VMEM((2, 2, cap, cl), BF16),
                pltpu.VMEM((2, 2, cap, cr), BF16),
                pltpu.VMEM((2, 2 * cap, d), BF16),
                pltpu.VMEM((2, 2 * cap, ff), BF16),
                pltpu.VMEM((RING, 2, cap, cl), BF16),
                pltpu.VMEM((RING, 2, cap, cr), BF16),
                pltpu.VMEM((2, 2, cap, cl), BF16),
                pltpu.VMEM((2, 2, cap, cr), BF16),
                pltpu.VMEM((4 * cap, td), BF16),
                pltpu.VMEM((td, d), F32),
                dma((3,)),
                dma((2, ff // NT)),
                dma((2, 4)),
                dma((2, 2)),
                dma((steps, 2)),
                dma((steps, 2)),
                dma((steps, 2)),
                dma((steps, 2)),
                dma((steps, 2)),
                dma((steps, 2)),
                dma((steps, 2)),
                dma((steps, 2)),
            ],
            compiler_params=pltpu.CompilerParams(collective_id=1, has_side_effects=True, vmem_limit_bytes=63 << 20),
            name="experts",
        )(n0, x, recvl, recvr, w1, w3, w2, h1, h3, h2, pc.reshape(steps, 2 * loc, td), gc, gt[0].reshape(td, 1))[0]
        return y

    spec_t = P(("dp", "ep"), None)
    spec_w = P("ep", None, None)
    return jax.shard_map(local, mesh=mesh, in_specs=(spec_t, spec_t, spec_t, spec_w, spec_w, spec_w), out_specs=spec_t, check_vma=False)
```

time: 753 us -> 633 us (0.84)
  Pallas kernels: 732 us -> 610 us
    pallas_call x1, Pallas kernels: 403 us -> 340 us  [local(): pl.pallas_call(functools.partial(experts_kernel, side, cap, loc), out_sha...]
    pallas_call x2 -> x1, Pallas kernels: 329 us -> 270 us  [local(): pl.pallas_call(functools.partial(dispatch_kernel, side, cap, loc), out_sh...]
  transfers between devices with their start and end apart: 1 -> 1, of which waited for: 0 -> 0; matrix products, arithmetic and copies ran while one was open for 1% -> 1% of each run, Pallas kernels for 44% -> 43%
where the time goes in v2:
time: 633 us; the launch traced here: 631 us
  Pallas kernels  610 us (96%)
  starting transfers between devices  8.31 us (1%)
  local copies, waits for them, and re-layouts  7.36 us (1%)
    pallas_call x1, Pallas kernels, local(): pl.pallas_call(functools.partial(experts_kernel, side, cap, loc), out_sha...  340 us
    pallas_call x1, Pallas kernels, local(): pl.pallas_call(functools.partial(dispatch_kernel, side, cap, loc), out_sh...  270 us
  transfers between devices with their start and end apart: 1, of which 0 were waited for; matrix products, arithmetic and copies ran while one was open for 1% of the time, Pallas kernels for 43%

profile of v2, /device:TPU:99, one launch (start us, length us, event | category | flops | bytes accessed | tf_op | source)
XLA Modules:
  0.0 630.9 jit_solution(8995527934486816547)
XLA Ops:
  0.0 0.9 fusion.1
  0.9 0.2 convert_reduce_fusion
  1.1 0.1 reshape.32
  1.2 0.6 slice_convert_fusion
  1.9 8.3 %all-to-all-start = ((s32[32,1,1]{2,1,0:T(1,128)}), s32[32,1,1]{2,1,0:T(1,128)S(1)}, u32[]{:S(2)}, u32[]{:S(2)}) async-start(s32[32,1,1]{2,1,0:T(1,128)} %bitcast), calls=%async_computation | async-start | bytes 32768 | tf_op jit(solution)/shard_map/all_to_all | solution.py:626
  10.2 0.7 convert_element_type.14
  10.9 0.9 select_reduce_fusion
  11.8 0.7 reshape.35.gt
  12.6 0.2 reduce_window_sum.13
  12.7 0.1 reduce_window_sum.14
  12.8 0.4 fusion.3
  13.3 0.1 reshape.34.ml
  13.4 0.0 copy-start
  13.4 0.7 reshape_reshape.3.pt
  14.1 0.7 copy.28
  14.8 0.9 copy.26.gh
  15.7 0.0 copy-done
  15.7 270.3 %dispatch.1 = (bf16[4,4,2,192,512]{4,3,2,1,0:T(8,128)(2,1)}, bf16[4,4,2,192,1536]{4,3,2,1,0:T(8,128)(2,1)}, bf16[2048,1024]{1,0:T(8,128)(2,1)}, bf16[2048,1024]{1,0:T(8,128)(2,1)}, bf16[1024,2048]{1,0:T(8,128)(2,1)}) custom-call(bf16[768,2048]{1,0:T(8,128)(2,1)} %x.3, f32[4,4,4,768]{3,2,1,0:T(4,128)} %copy-done, f32[4,4,4,768]{3,2,1,0:T(4,128)} %bitcast.11, ...), custom_call_target="tpu_custom_call" | custom-call | tf_op jit(solution)/shard_map/dispatch/pallas_call | solution.py:632
  286.0 0.0 all-to-all-done
  286.0 1.2 reduce.n0
  287.3 339.6 %experts.1 = (bf16[768,2048]{1,0:T(8,128)(2,1)}, bf16[16,2,192,512]{3,2,1,0:T(8,128)(2,1)}, bf16[16,2,192,1536]{3,2,1,0:T(8,128)(2,1)}, bf16[16,2,192,512]{3,2,1,0:T(8,128)(2,1)}, bf16[16,2,192,1536]{3,2,1,0:T(8,128)(2,1)}) custom-call(s32[32]{0:T(128)} %reduce.n0, bf16[768,2048]{1,0:T(8,128)(2,1)} %x.3, ...), custom_call_target="tpu_custom_call" | custom-call | tf_op jit(solution)/shard_map/experts/pallas_call | solution.py:663
  626.9 4.0 copy.30
  (3 shorter events, 0.0 us)
Async XLA Ops:
  1.9 284.2 %all-to-all-start = ((s32[32,1,1]{2,1,0:T(1,128)}), s32[32,1,1]{2,1,0:T(1,128)S(1)}, u32[]{:S(2)}, u32[]{:S(2)}) async-start(s32[32,1,1]{2,1,0:T(1,128)} %bitcast), calls=%async_computation | async-start | bytes 32768 | tf_op jit(solution)/shard_map/all_to_all | solution.py:626
  13.4 2.4 copy-start

commit v3 on v2

--- a/solution.py
+++ b/solution.py
@@ -18,8 +18,10 @@
 CT = 512
 WT = 512
 RING = 6
-LAG_F = 3
+LAG_F = 2
+HOT_AT = 5
 LAG_C = 8
+ORDER = ((2, 2), (3, 2), (2, 3), (3, 3), (1, 3), (3, 1), (1, 1), (0, 0), (1, 2), (2, 1), (2, 0), (0, 1), (3, 0), (0, 2), (1, 0), (0, 3))
 PARTS = 2
 
 
@@ -86,13 +88,13 @@
     def pass_on(self, src, dst, j):
         return remote(src, dst, self.sems[2].at[j], self.sems[3].at[j], self.mate)
 
-    def begin(self):
+    def begin(self, lo, hi):
         @pl.when(jnp.logical_and(self.lane, self.rel == 0))
         def _():
-            for pair in self.pieces:
+            for pair in self.pieces[lo:hi]:
                 for half, (w, h, rows, j) in enumerate(pair):
                     self.hop(w.at[self.slot, rows], h.at[rows], j, half).start()
-            for pair in self.pieces:
+            for pair in self.pieces[lo:hi]:
                 for w, h, rows, j in pair:
                     self.pass_on(w.at[self.slot, rows], h.at[rows], j).start()
 
@@ -174,7 +176,7 @@
         sends.append(remote(x.at[:, t["cols"]], t["xv"].at[1], ag_s.at[i, 1], ag_r.at[i, 1], along(a, last, at.c)))
     for cp in sends:
         cp.start()
-    chain.begin()
+    chain.begin(0, 1)
 
     def pack(t, k):
         there = at.x if t["axis"] == 0 else at.y
@@ -234,6 +236,7 @@
     pass_along(lside)
     pack(lside, last)
     pass_along(rside)
+    chain.begin(1, 3 * PARTS)
     pack(rside, last)
     pack(lside, 1)
     send(rside, last)
@@ -245,18 +248,19 @@
         cp.wait_recv()
     pack(lside, 2)
     chain.serve(2)
-    send(lside, last)
     chain.serve(3)
     for cp in fwd[1]:
         cp.wait_recv()
     pack(rside, 2)
     chain.serve(4)
     send(rside, 2)
+    send(lside, last)
+    chain.serve(5)
     send(lside, 1)
-    chain.serve(5)
     chain.serve(6)
+    chain.serve(7)
     send(lside, 2)
-    for n in range(7, chain.slots + 1):
+    for n in range(8, chain.slots + 1):
         chain.serve(n)
     for cp in sends + fwd[0] + fwd[1]:
         cp.wait_send()
@@ -281,24 +285,25 @@
     side, cap, slot_last, n0, x, recvl, recvr, w1, w3, w2, h1, h3, h2, pt, gt, gh,
     y, rell, relr, retl, retr,
     w1v, w3v, w2v, xbl, xbr, xs, av, ol, orr, ocl, ocr, gm, yacc,
-    w_sem, u_sem, x_sem, c_sem, s1l, s1r, r1l, r1r, s2l, s2r, r2l, r2r,
+    w_sem, u_sem, x_sem, c_sem, k_sem, s1l, s1r, r1l, r1r, s2l, s2r, r2l, r2r,
 ):
     at = Place(side)
     td = x.shape[0]
-    cl, cr = ol.shape[3], orr.shape[3]
+    cl, cr = xbl.shape[3], xbr.shape[3]
+    co = ol.shape[3]
     d_model, ff = w1.shape[1], w1.shape[2]
     steps = side * side
-    n_rel = (side - 1) * (side - 1)
     m2 = 2 * cap
 
+    words = [sum(o[i] << (2 * n) for n, o in enumerate(ORDER)) for i in range(2)]
+    words = [w - (1 << 32) if w >= 1 << 31 else w for w in words]
+
     def where_to(s):
-        b = lax.div(s, n_rel)
-        t = s - b * n_rel
-        r, q = lax.rem(t, 3), lax.div(t, 3)
-        e, f = lax.rem(t, 2), lax.div(t, 2)
-        dx = (1 - b) * (1 + r) + b * (1 - e) * (1 + f)
-        dy = (1 - b) * (1 + lax.rem(r + q, 3)) + b * e * (1 + f)
-        return lax.rem(dy, side), lax.rem(dx, side)
+        return tuple(lax.bitwise_and(lax.shift_right_logical(jnp.int32(w), 2 * s), jnp.int32(3)) for w in words)
+
+    def kind(s):
+        dy, dx = where_to(s)
+        return dy * dx > 0, dy + dx == 0
 
     def load_w(w, v, i):
         return pltpu.make_async_copy(w, v, w_sem.at[i])
@@ -339,40 +344,46 @@
             relay.append(remote(o.at[so, j], rel.at[s, j], s1.at[s, j], r1.at[s, j], via))
             direct.append(remote(o.at[so, j], ret.at[s, at.c], s1.at[s, j], r2.at[s, at.c], at.dev(dy, dx, j)))
         mate = remote(o.at[so, 1 - at.c], ret.at[s, at.c], s1.at[s, 0], r2.at[s, at.c], at.dev(0, 0, 1 - at.c))
-        self_cp = keep(o.at[so, at.c], ret.at[s, at.c], r2.at[s, at.c])
+        self_cp = keep(o.at[so, at.c], ret.at[s, at.c], k_sem.at[h])
         return relay, direct, mate, self_cp
 
     def start_first(s):
         hops = [first_hop(s, h) for h in range(2)]
 
-        @pl.when(s < n_rel)
+        by_relay, stay = kind(s)
+
+        @pl.when(by_relay)
         def _():
             for relay, *_ in hops:
                 for cp in relay:
                     cp.start()
 
-        @pl.when(jnp.logical_and(s >= n_rel, s < steps - 1))
+        @pl.when(jnp.logical_not(jnp.logical_or(by_relay, stay)))
         def _():
             for _, direct, *_ in hops:
                 for cp in direct:
                     cp.start()
 
-        @pl.when(s == steps - 1)
+        @pl.when(stay)
         def _():
             for *_, mate, self_cp in hops:
                 mate.start()
                 self_cp.start()
+            for *_, self_cp in hops:
+                self_cp.wait()
 
     def wait_first(s):
         hops = [first_hop(s, h) for h in range(2)]
 
-        @pl.when(s < steps - 1)
+        stay = kind(s)[1]
+
+        @pl.when(jnp.logical_not(stay))
         def _():
             for _, direct, *_ in hops:
                 for cp in direct:
                     cp.wait_send()
 
-        @pl.when(s == steps - 1)
+        @pl.when(stay)
         def _():
             for *_, mate, _ in hops:
                 mate.wait_send()
@@ -387,10 +398,12 @@
         return got, on
 
     def forward(s):
-        for h in range(2):
-            for cp, on in zip(*second_hop(s, h)):
-                cp.wait_recv()
-                on.start()
+        @pl.when(kind(s)[0])
+        def _():
+            for h in range(2):
+                for cp, on in zip(*second_hop(s, h)):
+                    cp.wait_recv()
+                    on.start()
 
     def fetch(p):
         for i in range(2):
@@ -398,7 +411,12 @@
             for h, oc in enumerate((ocl, ocr)):
                 o, rel, ret, s1, r1, s2, r2 = halves[h]
                 for c in range(2):
-                    remote(ret.at[s, c], ret.at[s, c], s2.at[s, c], r2.at[s, c], at.dev(0, 1, at.c)).wait_recv()
+                    mine = jnp.logical_and(kind(s)[1], at.c == c)
+
+                    @pl.when(jnp.logical_not(mine))
+                    def _():
+                        remote(ret.at[s, c], ret.at[s, c], s2.at[s, c], r2.at[s, c], at.dev(0, 1, at.c)).wait_recv()
+
                 pltpu.make_async_copy(ret.at[s], oc.at[i], c_sem.at[h, i]).start()
 
     def combine(p):
@@ -418,16 +436,15 @@
         for h, oc in enumerate((ocl, ocr)):
             for i in range(2):
                 pltpu.make_async_copy(halves[h][2].at[2 * p + i], oc.at[i], c_sem.at[h, i]).wait()
-            width = cl if h == 0 else cr
 
             def col(n, carry):
                 cols = pl.ds(pl.multiple_of(n * CT, CT), CT)
-                to = pl.ds(pl.multiple_of(h * cl + n * CT, CT), CT)
+                to = pl.ds(pl.multiple_of(h * co + n * CT, CT), CT)
                 b = oc[:, :, :, cols].reshape(2 * m2, CT)
                 yacc[:, to] += lax.dot_general(gm[...], b, (((0,), (0,)), ((), ())), preferred_element_type=F32)
                 return carry
 
-            lax.fori_loop(0, width // CT, col, 0)
+            lax.fori_loop(0, co // CT, col, 0)
 
     def step(s, carry):
         slot, so = lax.rem(s, 2), lax.rem(s, RING)
@@ -477,7 +494,7 @@
         def _():
             wait_first(s - RING)
 
-        for o, lo, width in ((ol, 0, cl), (orr, cl, cr)):
+        for o, lo in ((ol, 0), (orr, co)):
 
             def down(n, carry):
                 to = pl.ds(pl.multiple_of(n * WT, WT), WT)
@@ -486,9 +503,9 @@
                 o[so, :, :, to] = r.astype(BF16).reshape(2, cap, WT)
                 return carry
 
-            lax.fori_loop(0, width // WT, down, 0)
-
-        @pl.when(jnp.logical_and(s >= LAG_F, s - LAG_F < n_rel))
+            lax.fori_loop(0, co // WT, down, 0)
+
+        @pl.when(s >= LAG_F)
         def _():
             forward(s - LAG_F)
 
@@ -507,6 +524,8 @@
         return carry
 
     lax.fori_loop(0, steps, step, 0)
+    for s in range(steps - LAG_F, steps):
+        forward(s)
 
     is_h = jnp.logical_and(at.x == lax.rem(at.y, 2), at.c == lax.div(at.y, 2))
     hs = lax.div(at.y + side - 1, side) * slot_last
@@ -535,8 +554,8 @@
         combine(p)
         return carry
 
-    lax.fori_loop(begun, steps // 2 - 2, drain, 0)
-    fetch(steps // 2 - 2)
+    lax.fori_loop(begun, HOT_AT, drain, 0)
+    fetch(HOT_AT)
     for i, (h, v) in enumerate(((h1, w1v), (h3, w3v), (h2, w2v))):
         load_w(h, v.at[0], i).wait()
     for i in range(td // m2):
@@ -560,8 +579,8 @@
 
         lax.fori_loop(0, d_model // WT, down1, 0)
 
-    combine(steps // 2 - 2)
-    drain(steps // 2 - 1, 0)
+    combine(HOT_AT)
+    lax.fori_loop(HOT_AT + 1, steps // 2, drain, 0)
 
     def out(n, carry):
         cols = pl.ds(pl.multiple_of(n * NT, NT), NT)
@@ -581,12 +600,15 @@
     lax.fori_loop(steps - RING, steps, settle, 0)
 
     def settle2(s, carry):
-        for h in range(2):
-            for cp in second_hop(s, h)[1]:
-                cp.wait_send()
+        @pl.when(kind(s)[0])
+        def _():
+            for h in range(2):
+                for cp in second_hop(s, h)[1]:
+                    cp.wait_send()
+
         return carry
 
-    lax.fori_loop(0, n_rel, settle2, 0)
+    lax.fori_loop(0, steps, settle2, 0)
     for cp in done:
         cp.wait()
 
@@ -659,10 +681,10 @@
         )(x, ml, mr, w1, w3, w2)
 
         steps = side * side
-        blocks = [jax.ShapeDtypeStruct((steps, 2, cap, c), BF16) for c in (cl, cr)]
+        block = [jax.ShapeDtypeStruct((steps, 2, cap, d // 2), BF16)]
         y = pl.pallas_call(
             functools.partial(experts_kernel, side, cap, loc),
-            out_shape=[jax.ShapeDtypeStruct((td, d), BF16)] + blocks + blocks,
+            out_shape=[jax.ShapeDtypeStruct((td, d), BF16)] + 4 * block,
             in_specs=[SMEM] + [ANY] * 9 + [VMEM] * 3,
             out_specs=[ANY] * 5,
             scratch_shapes=[
@@ -673,16 +695,17 @@
                 pltpu.VMEM((2, 2, cap, cr), BF16),
                 pltpu.VMEM((2, 2 * cap, d), BF16),
                 pltpu.VMEM((2, 2 * cap, ff), BF16),
-                pltpu.VMEM((RING, 2, cap, cl), BF16),
-                pltpu.VMEM((RING, 2, cap, cr), BF16),
-                pltpu.VMEM((2, 2, cap, cl), BF16),
-                pltpu.VMEM((2, 2, cap, cr), BF16),
+                pltpu.VMEM((RING, 2, cap, d // 2), BF16),
+                pltpu.VMEM((RING, 2, cap, d // 2), BF16),
+                pltpu.VMEM((2, 2, cap, d // 2), BF16),
+                pltpu.VMEM((2, 2, cap, d // 2), BF16),
                 pltpu.VMEM((4 * cap, td), BF16),
                 pltpu.VMEM((td, d), F32),
                 dma((3,)),
                 dma((2, ff // NT)),
                 dma((2, 4)),
                 dma((2, 2)),
+                dma((2,)),
                 dma((steps, 2)),
                 dma((steps, 2)),
                 dma((steps, 2)),

time: 633 us -> 582 us (0.919)
  Pallas kernels: 610 us -> 557 us
    pallas_call x1, Pallas kernels: 340 us -> 311 us  [local(): pl.pallas_call(functools.partial(experts_kernel, side, cap, loc), out_sha...]
    pallas_call x1, Pallas kernels: 270 us -> 246 us  [local(): pl.pallas_call(functools.partial(dispatch_kernel, side, cap, loc), out_sh...]
where the time goes in v3:
time: 582 us; the launch traced here: 578 us
  Pallas kernels  557 us (96%)
  starting transfers between devices  8.31 us (1%)
  local copies, waits for them, and re-layouts  7.36 us (1%)
    pallas_call x1, Pallas kernels, local(): pl.pallas_call(functools.partial(experts_kernel, side, cap, loc), out_sha...  311 us
    pallas_call x1, Pallas kernels, local(): pl.pallas_call(functools.partial(dispatch_kernel, side, cap, loc), out_sh...  246 us
  transfers between devices with their start and end apart: 1, of which 0 were waited for; matrix products, arithmetic and copies ran while one was open for 1% of the time, Pallas kernels for 43%

profile of v3, /device:TPU:99, one launch (start us, length us, event | category | flops | bytes accessed | tf_op | source)
XLA Modules:
  0.0 577.6 jit_solution(8408666240079976332)
XLA Ops:
  0.0 0.9 fusion.1
  0.9 0.2 convert_reduce_fusion
  1.1 0.1 reshape.32
  1.2 0.6 slice_convert_fusion
  1.9 8.3 %all-to-all-start = ((s32[32,1,1]{2,1,0:T(1,128)}), s32[32,1,1]{2,1,0:T(1,128)S(1)}, u32[]{:S(2)}, u32[]{:S(2)}) async-start(s32[32,1,1]{2,1,0:T(1,128)} %bitcast), calls=%async_computation | async-start | bytes 32768 | tf_op jit(solution)/shard_map/all_to_all | solution.py:648
  10.2 0.7 convert_element_type.14
  10.9 0.9 select_reduce_fusion
  11.8 0.7 reshape.35.gt
  12.6 0.2 reduce_window_sum.13
  12.7 0.1 reduce_window_sum.14
  12.8 0.4 fusion.3
  13.3 0.1 reshape.34.ml
  13.4 0.0 copy-start
  13.4 0.7 reshape_reshape.3.pt
  14.1 0.7 copy.28
  14.8 0.9 copy.26.gh
  15.7 0.0 copy-done
  15.7 245.5 %dispatch.1 = (bf16[4,4,2,192,512]{4,3,2,1,0:T(8,128)(2,1)}, bf16[4,4,2,192,1536]{4,3,2,1,0:T(8,128)(2,1)}, bf16[2048,1024]{1,0:T(8,128)(2,1)}, bf16[2048,1024]{1,0:T(8,128)(2,1)}, bf16[1024,2048]{1,0:T(8,128)(2,1)}) custom-call(bf16[768,2048]{1,0:T(8,128)(2,1)} %x.3, f32[4,4,4,768]{3,2,1,0:T(4,128)} %copy-done, f32[4,4,4,768]{3,2,1,0:T(4,128)} %bitcast.11, ...), custom_call_target="tpu_custom_call" | custom-call | tf_op jit(solution)/shard_map/dispatch/pallas_call | solution.py:654
  261.3 0.0 all-to-all-done
  261.3 1.2 reduce.n0
  262.5 311.1 %experts.1 = (bf16[768,2048]{1,0:T(8,128)(2,1)}, bf16[16,2,192,1024]{3,2,1,0:T(8,128)(2,1)}, bf16[16,2,192,1024]{3,2,1,0:T(8,128)(2,1)}, bf16[16,2,192,1024]{3,2,1,0:T(8,128)(2,1)}, bf16[16,2,192,1024]{3,2,1,0:T(8,128)(2,1)}) custom-call(s32[32]{0:T(128)} %reduce.n0, bf16[768,2048]{1,0:T(8,128)(2,1)} %x.3, ...), custom_call_target="tpu_custom_call" | custom-call | tf_op jit(solution)/shard_map/experts/pallas_call | solution.py:685
  573.6 4.0 copy.30
  (3 shorter events, 0.0 us)
Async XLA Ops:
  1.9 259.4 %all-to-all-start = ((s32[32,1,1]{2,1,0:T(1,128)}), s32[32,1,1]{2,1,0:T(1,128)S(1)}, u32[]{:S(2)}, u32[]{:S(2)}) async-start(s32[32,1,1]{2,1,0:T(1,128)} %bitcast), calls=%async_computation | async-start | bytes 32768 | tf_op jit(solution)/shard_map/all_to_all | solution.py:648
  13.4 2.4 copy-start

commit v4 on v3

v4 whole, which is shorter than its diff:
```python
import functools
import math

import jax
import jax.numpy as jnp
from jax import lax
from jax.experimental import pallas as pl
from jax.experimental.pallas import tpu as pltpu
from jax.sharding import PartitionSpec as P

MESH = pl.DeviceIdType.MESH
ANY = pl.BlockSpec(memory_space=pl.ANY)
VMEM = pl.BlockSpec(memory_space=pltpu.VMEM)
F32 = jnp.float32
BF16 = jnp.bfloat16
NT = 256
CT = 512
WT = 512
RING = 6
LAG_F = 3
HOT_AT = 5
LAG_C = 10
ORDER = ((0, 0), (0, 1), (0, 3), (1, 1), (2, 0), (0, 2), (2, 1), (3, 1), (1, 3), (2, 3), (3, 0), (1, 2), (1, 0), (3, 2), (2, 2), (3, 3))
WAIT = 2
PARTS = 4


def holder_list(p):
    return [0, (p // 2 + 1) % p, (p // 4 + 2) % p, (3 * p // 4 + 3) % p]


class Place:
    def __init__(self, side):
        me = lax.axis_index("ep")
        self.side = side
        self.z = lax.axis_index("dp")
        self.c = lax.rem(me, 2)
        self.x = lax.rem(lax.div(me, 2), side)
        self.y = lax.div(me, 2 * side)

    def index(self, dy, dx, c):
        s = self.side
        return (lax.rem(self.y + dy, s) * s + lax.rem(self.x + dx, s)) * 2 + c

    def dev(self, dy, dx, c):
        return (self.z, self.index(dy, dx, c))

    def greet(self):
        bar = pltpu.get_barrier_semaphore()
        near = [self.dev(0, 0, 1 - self.c)]
        for k in range(1, self.side):
            for c in range(2):
                near += [self.dev(0, k, c), self.dev(k, 0, c)]
        for d in near:
            pl.semaphore_signal(bar, inc=1, device_id=d, device_id_type=MESH)
        pl.semaphore_wait(bar, len(near))


def remote(src, dst, ssem, rsem, dev):
    return pltpu.make_async_remote_copy(src_ref=src, dst_ref=dst, send_sem=ssem, recv_sem=rsem, device_id=dev, device_id_type=MESH)


def keep(src, dst, sem):
    return pltpu.make_async_copy(src, dst, sem)


class Chain:
    def __init__(self, at, loc, pairs, s_sem, r_sem, p_sem, q_sem):
        side = self.side = at.side
        hx, hc = lax.rem(at.y, 2), lax.div(at.y, 2)
        rel = lax.rem(at.x + side - hx, side)
        self.hops = (rel, lax.rem(side - rel, side))
        self.slot = lax.div(at.y + side - 1, side) * loc
        self.c = at.c
        self.holder = jnp.logical_and(at.c == hc, rel == 0)
        self.beside = jnp.logical_and(at.c != hc, rel == 0)
        self.next = (at.dev(0, 1, at.c), at.dev(0, side - 1, at.c))
        self.mate = at.dev(0, 0, 1 - at.c)
        self.pairs = pairs
        self.sems = s_sem, r_sem, p_sem, q_sem
        self.turns = len(pairs) * PARTS + WAIT * (side - 1)

    def part(self, m, i, half, core):
        w, h = self.pairs[m]
        n = w.shape[1] // (4 * PARTS)
        rows, j = pl.ds(((half * 2 + core) * PARTS + i) * n, n), ((m * PARTS + i) * 2 + half) * 2 + core
        hop = lambda src: remote(src, h.at[rows], self.sems[0].at[j], self.sems[1].at[j], self.next[half])
        on = lambda src: remote(src, h.at[rows], self.sems[2].at[j], self.sems[3].at[j], self.mate)
        return w.at[self.slot, rows], h.at[rows], hop, on

    def every(self, do):
        def each(i, carry):
            for half, hops in enumerate(self.hops):
                for m in range(len(self.pairs)):
                    do(m, i, half, hops)
            return carry

        lax.fori_loop(0, PARTS, each, 0)

    def begin(self):
        @pl.when(self.holder)
        def _():
            def give(m, i, half, hops):
                own, _, _, on = self.part(m, i, half, 1 - self.c)
                on(own).start()

            self.every(give)

    def serve(self, turn):
        for half, hops in enumerate(self.hops):
            for m in range(len(self.pairs)):
                i = turn - WAIT * hops - m * PARTS

                @pl.when(jnp.logical_and(i >= 0, i < PARTS))
                def _():
                    own, got, hop, on = self.part(m, i, half, self.c)

                    @pl.when(self.holder)
                    def _():
                        hop(own).start()
                        on(own).start()

                    @pl.when(self.beside)
                    def _():
                        on(got).wait_recv()
                        hop(got).start()

                    @pl.when(hops > 0)
                    def _():
                        hop(got).wait_recv()

                        @pl.when(hops < self.side - 1)
                        def _():
                            hop(got).start()

                        on(got).start()

    def finish(self):
        def settle(m, i, half, hops):
            _, got, hop, on = self.part(m, i, half, self.c)
            _, got2, _, on2 = self.part(m, i, half, 1 - self.c)

            @pl.when(hops < self.side - 1)
            def _():
                hop(got).wait_send()

            @pl.when(jnp.logical_not(self.beside))
            def _():
                on(got).wait_send()

            @pl.when(self.holder)
            def _():
                on2(got2).wait_send()

            @pl.when(jnp.logical_not(self.holder))
            def _():
                on2(got2).wait_recv()

        self.every(settle)


def layer_kernel(
    side, cap, loc, x, ml, mr, w1, w3, w2, pt, gt, gh,
    y, xlh, xrh, sbl, sbr, recvl, recvr, h1, h3, h2, rell, relr, retl, retr,
    mlv, mrv, sel, cntb, nrec, w1v, w3v, w2v, xbl, xbr, xs, av, ob, ocl, ocr, gm, yacc,
    m_s, m_r, ag_s, ag_r, xk, st, own, n_s, n_r, s_l, r_l, s_r, r_r,
    w_sem, x_sem, c_sem, k_sem, s1l, s1r, r1l, r1r, s2l, s2r, r2l, r2r, *w_sems,
):
    at = Place(side)
    chain = Chain(at, loc, ((w1, h1), (w3, h3), (w2, h2)), *w_sems)
    td, d_model = x.shape
    ff = w1.shape[2]
    cl, cr = xbl.shape[3], xbr.shape[3]
    co = d_model // 2
    steps = side * side
    m2 = 2 * cap
    half, last = td // 2, side - 1
    lside, rside = sides = (
        dict(i=0, axis=0, lo=0, width=cl, xh=xlh, m=ml, mv=mlv, sb=sbl, rv=recvl, ss=s_l, rs=r_l),
        dict(i=1, axis=1, lo=cl, width=cr, xh=xrh, m=mr, mv=mrv, sb=sbr, rv=recvr, ss=s_r, rs=r_r),
    )

    def along(a, k, c):
        return at.dev(k, 0, c) if a == 0 else at.dev(0, k, c)


    mine = [pltpu.make_async_copy(t["m"].at[at.y if t["axis"] == 0 else at.x], t["mv"].at[0], own.at[t["i"]]) for t in sides]
    for cp in mine:
        cp.start()
    rows0 = pltpu.make_async_copy(x, xs, xk.at[0])
    rows0.start()
    at.greet()
    sends = []
    for t in sides:
        i, a, here = t["i"], t["axis"], at.y if t["axis"] == 0 else at.x
        for k in range(1, side):
            sends.append(remote(t["m"].at[lax.rem(here + k, side)], t["mv"].at[side - k], m_s.at[i, k], m_r.at[i, side - k], along(a, k, at.c)))
        src = x.at[:, pl.ds(t["lo"], t["width"])]
        sends.append(remote(src, t["xh"].at[last], ag_s.at[i, 0], ag_r.at[i, last], along(a, 1, at.c)))
        sends.append(remote(src, t["xh"].at[1], ag_s.at[i, 1], ag_r.at[i, 1], along(a, last, at.c)))
    for cp in sends:
        cp.start()
    weights = [pltpu.make_async_copy(w.at[pl.ds(0, 2)], v, w_sem.at[i]) for i, (w, v) in enumerate(((w1, w1v), (w3, w3v), (w2, w2v)))]
    for cp in weights:
        cp.start()


    def staged(t, k, d):
        cols = pl.ds(t["lo"], t["width"])
        slot = (k, 0, at.c) if t["axis"] == 0 else (0, k, at.c)
        both = pltpu.make_async_copy(ob.at[d, :, :, cols], t["sb"].at[k, d], st.at[t["i"], d])
        other = pltpu.make_async_copy(ob.at[d, 1 - at.c, :, cols], t["sb"].at[k, d, 1 - at.c], st.at[t["i"], d])
        self_ = pltpu.make_async_copy(ob.at[d, at.c, :, cols], t["rv"].at[slot], own.at[t["i"]])
        return both, other, self_

    def pack(k):
        def one(d, carry):
            r = lax.broadcasted_iota(jnp.int32, (cap, td), 0).astype(F32)
            for t in sides:
                q = lax.rem((at.x if t["axis"] == 0 else at.y) + d, side)
                for c in range(2):
                    p0 = t["mv"][k, q, 2 * c : 2 * c + 1, :]
                    p1 = t["mv"][k, q, 2 * c + 1 : 2 * c + 2, :]
                    hit = jnp.logical_or(r == p0, r == p1)
                    sel[c * cap : (c + 1) * cap, :] = jnp.where(hit, 1.0, 0.0).astype(BF16)

                def col(n, carry):
                    cols = pl.ds(pl.multiple_of(t["lo"] + n * WT, WT), WT)
                    o = jnp.dot(sel[...], xs[:, cols], preferred_element_type=F32).astype(BF16)
                    ob[d, :, :, cols] = o.reshape(2, cap, WT)
                    return carry

                lax.fori_loop(0, t["width"] // WT, col, 0)
            for t in sides:
                both, other, self_ = staged(t, k, d)

                @pl.when(d > 0)
                def _():
                    both.start()

                @pl.when(d == 0)
                def _():
                    other.start()
                    self_.start()

            return carry

        lax.fori_loop(0, side, one, 0)

    def stored(k):
        for t in sides:
            for d in range(side):
                both, other, self_ = staged(t, k, d)
                if d:
                    both.wait()
                else:
                    other.wait()
                    self_.wait()

    def block(t, k, d, c):
        to = (side - d) % side
        slot = (k, to, at.c) if t["axis"] == 0 else (to, k, at.c)
        return remote(t["sb"].at[k, d, c], t["rv"].at[slot], t["ss"].at[k, d, c], t["rs"].at[slot], along(1 - t["axis"], d, c))

    def send(t, k):
        block(t, k, 0, 1 - at.c).start()
        for d in (1, side - 1, 2):
            for c in range(2):
                block(t, k, d, c).start()

    fwd = {}

    def pass_along(t):
        i, a, xh = t["i"], t["axis"], t["xh"]
        fwd[i] = []
        for k, rows, to in ((last, pl.ds(0, half), 1), (1, pl.ds(half, half), last)):
            remote(xh.at[k], xh.at[k], ag_s.at[i, 0], ag_r.at[i, k], along(a, 1, at.c)).wait_recv()
            cp = remote(xh.at[k, rows], xh.at[2, rows], ag_s.at[i, 2 if to == 1 else 3], ag_r.at[i, 2 if to == 1 else 0], along(a, to, at.c))
            cp.start()
            fwd[i].append(cp)
        for k in range(1, side):
            remote(t["mv"].at[k], t["mv"].at[k], m_s.at[i, k], m_r.at[i, k], along(a, 1, at.c)).wait_recv()

    def take(k):
        cps = [pltpu.make_async_copy(t["xh"].at[k], xs.at[:, pl.ds(t["lo"], t["width"])], xk.at[t["i"]]) for t in sides]
        for cp in cps:
            cp.start()
        for cp in cps:
            cp.wait()

    def count_send(d, c):
        return remote(cntb.at[d, c], nrec.at[(side - d) % side, at.c], n_s.at[d, c], n_r.at[(side - d) % side, at.c], along(1, d, c))

    for cp in mine:
        cp.wait()
    rows0.wait()
    pack(0)
    yacc[...] = jnp.zeros_like(yacc)
    stored(0)
    send(rside, 0)
    pass_along(lside)
    for d in range(side):
        for c in range(2):
            for k in range(side):
                q = lax.rem(at.x + d, side)
                n = jnp.sum(jnp.where(mlv[k, q, 2 * c : 2 * c + 1, :] >= 0.0, 1.0, 0.0), axis=1, keepdims=True)
                cntb[d, c, k] = jnp.broadcast_to(n, cntb.shape[3:])
    nrec[0, at.c] = cntb[0, at.c]
    pass_along(rside)
    chain.begin()
    chain.serve(0)
    send(lside, 0)
    count_send(0, 1 - at.c).start()
    for d in range(1, side):
        for c in range(2):
            count_send(d, c).start()
    for k in (last, 1):
        take(k)
        pack(k)
        stored(k)
        send(rside, k)
        send(lside, k)
        chain.serve(1 if k == last else 2)
    for i in range(2):
        for cp in fwd[i]:
            cp.wait_recv()
    take(2)
    pack(2)
    stored(2)
    send(rside, 2)
    send(lside, 2)


    words = [sum(o[i] << (2 * n) for n, o in enumerate(ORDER)) for i in range(2)]
    words = [w - (1 << 32) if w >= 1 << 31 else w for w in words]

    def where_to(s):
        return tuple(lax.bitwise_and(lax.shift_right_logical(jnp.int32(w), 2 * s), jnp.int32(3)) for w in words)

    def kind(s):
        dy, dx = where_to(s)
        return dy * dx > 0, dy + dx == 0

    def ends(s):
        dy, dx = where_to(s)
        return (dy, dx), (lax.rem(side - dy, side), lax.rem(side - dx, side))

    def load_x(s):
        slot = lax.rem(s, 2)
        return [
            pltpu.make_async_copy(t["rv"].at[dy, dx, j], xb.at[slot, j], x_sem.at[slot, 2 * t["i"] + j])
            for j, (dy, dx) in enumerate(ends(s))
            for t, xb in zip(sides, (xbl, xbr))
        ]

    def arrive(s):
        for j, (dy, dx) in enumerate(ends(s)):
            for t in sides:
                rv = t["rv"].at[dy, dx, j]
                here = jnp.logical_and((dx if t["axis"] == 0 else dy) == 0, at.c == j)

                @pl.when(jnp.logical_not(here))
                def _():
                    remote(rv, rv, t["ss"].at[0, 0, 0], t["rs"].at[dy, dx, j], along(0, 1, at.c)).wait_recv()

        for cp in load_x(s):
            cp.start()

    outs = (pl.ds(0, co), pl.ds(co, co))
    halves = ((rell, retl, s1l, r1l, s2l, r2l), (relr, retr, s1r, r1r, s2r, r2r))

    def first_hop(s, h):
        rel, ret, s1, r1, s2, r2 = halves[h]
        so = lax.rem(s, RING)
        relay, direct = [], []
        for j, (dy, dx) in enumerate(ends(s)):
            via = at.dev(0, dx, at.c) if h == 0 else at.dev(dy, 0, at.c)
            src = ob.at[so, j, :, outs[h]]
            relay.append(remote(src, rel.at[s, j], s1.at[s, j], r1.at[s, j], via))
            direct.append(remote(src, ret.at[s, at.c], s1.at[s, j], r2.at[s, at.c], at.dev(dy, dx, j)))
        mate = remote(ob.at[so, 1 - at.c, :, outs[h]], ret.at[s, at.c], s1.at[s, 0], r2.at[s, at.c], at.dev(0, 0, 1 - at.c))
        self_cp = keep(ob.at[so, at.c, :, outs[h]], ret.at[s, at.c], k_sem.at[h])
        return relay, direct, mate, self_cp

    def start_first(s):
        hops = [first_hop(s, h) for h in range(2)]
        by_relay, stay = kind(s)

        @pl.when(by_relay)
        def _():
            for relay, *_ in hops:
                for cp in relay:
                    cp.start()

        @pl.when(jnp.logical_not(jnp.logical_or(by_relay, stay)))
        def _():
            for _, direct, *_ in hops:
                for cp in direct:
                    cp.start()

        @pl.when(stay)
        def _():
            for *_, mate, self_cp in hops:
                mate.start()
                self_cp.start()
            for *_, self_cp in hops:
                self_cp.wait()

    def wait_first(s):
        hops = [first_hop(s, h) for h in range(2)]
        stay = kind(s)[1]

        @pl.when(jnp.logical_not(stay))
        def _():
            for _, direct, *_ in hops:
                for cp in direct:
                    cp.wait_send()

        @pl.when(stay)
        def _():
            for *_, mate, _ in hops:
                mate.wait_send()

    def second_hop(s, h):
        rel, ret, s1, r1, s2, r2 = halves[h]
        got, on = [], []
        for j, (dy, dx) in enumerate(ends(s)):
            got.append(remote(rel.at[s, j], rel.at[s, j], s1.at[s, j], r1.at[s, j], at.dev(0, 1, at.c)))
            to = at.dev(dy, 0, j) if h == 0 else at.dev(0, dx, j)
            on.append(remote(rel.at[s, j], ret.at[s, at.c], s2.at[s, j], r2.at[s, at.c], to))
        return got, on

    def forward(s):
        @pl.when(kind(s)[0])
        def _():
            for h in range(2):
                for cp, on in zip(*second_hop(s, h)):
                    cp.wait_recv()
                    on.start()

    def fetch(p):
        for i in range(2):
            s = 2 * p + i
            for h, oc in enumerate((ocl, ocr)):
                rel, ret, s1, r1, s2, r2 = halves[h]
                for c in range(2):
                    here = jnp.logical_and(kind(s)[1], at.c == c)

                    @pl.when(jnp.logical_not(here))
                    def _():
                        remote(ret.at[s, c], ret.at[s, c], s2.at[s, c], r2.at[s, c], at.dev(0, 1, at.c)).wait_recv()

                pltpu.make_async_copy(ret.at[s], oc.at[i], c_sem.at[h, i]).start()

    def combine(p):
        for i in range(2):
            dy, dx = where_to(2 * p + i)
            oy = at.c * dy + (1 - at.c) * (side - dy)
            ox = at.c * dx + (1 - at.c) * (side - dx)
            chip = lax.rem(at.y + oy, side) * side + lax.rem(at.x + ox, side)
            r = lax.broadcasted_iota(jnp.int32, (cap, td), 0).astype(F32)
            for c in range(2):
                g = jnp.zeros((cap, td), F32)
                for j in range(2):
                    row = 2 * c + j
                    g = g + jnp.where(r == pt[chip, row : row + 1, :], gt[chip, row : row + 1, :], 0.0)
                lo = (2 * i + c) * cap
                gm[lo : lo + cap, :] = g.astype(BF16)
        for h, oc in enumerate((ocl, ocr)):
            for i in range(2):
                pltpu.make_async_copy(halves[h][1].at[2 * p + i], oc.at[i], c_sem.at[h, i]).wait()

            def col(n, carry):
                cols = pl.ds(pl.multiple_of(n * CT, CT), CT)
                to = pl.ds(pl.multiple_of(h * co + n * CT, CT), CT)
                b = oc[:, :, :, cols].reshape(2 * m2, CT)
                yacc[:, to] += lax.dot_general(gm[...], b, (((0,), (0,)), ((), ())), preferred_element_type=F32)
                return carry

            lax.fori_loop(0, co // CT, col, 0)

    for d in range(side):
        for c in range(2):
            if d:
                remote(nrec.at[d, c], nrec.at[d, c], n_s.at[d, c], n_r.at[d, c], along(1, 1, at.c)).wait_recv()
    remote(nrec.at[0, 1 - at.c], nrec.at[0, 1 - at.c], n_s.at[0, 0], n_r.at[0, 1 - at.c], along(1, 1, at.c)).wait_recv()
    for cp in weights:
        cp.wait()
    arrive(0)

    def step(s, carry):
        slot, so = lax.rem(s, 2), lax.rem(s, RING)
        for cp in load_x(s):
            cp.wait()
        cuts = [jnp.max(nrec[dx, j, dy]) for j, (dy, dx) in enumerate(ends(s))]
        for c in range(2):
            for xb, lo, width in ((xbl, 0, cl), (xbr, cl, cr)):
                for n in range(width // NT):
                    v = xb[slot, c, :, n * NT : (n + 1) * NT].astype(F32)
                    first = lax.broadcasted_iota(jnp.int32, (cap, NT), 0).astype(F32) < cuts[c]
                    z = jnp.zeros_like(v)
                    to = slice(lo + n * NT, lo + (n + 1) * NT)
                    xs[c * cap : (c + 1) * cap, to] = jnp.where(first, v, z).astype(BF16)
                    xs[m2 + c * cap : m2 + (c + 1) * cap, to] = jnp.where(first, z, v).astype(BF16)

        def up2(f, carry):
            cols = pl.ds(pl.multiple_of(f * NT, NT), NT)
            u = sum(jnp.dot(xs[e * m2 : (e + 1) * m2, :], w1v[e, :, cols], preferred_element_type=F32) for e in range(2))
            v = sum(jnp.dot(xs[e * m2 : (e + 1) * m2, :], w3v[e, :, cols], preferred_element_type=F32) for e in range(2))
            a = (jax.nn.silu(u) * v).astype(BF16).astype(F32)
            row = lax.broadcasted_iota(jnp.int32, (cap, NT), 0).astype(F32)
            first = jnp.concatenate([jnp.where(row < cuts[c], 1.0, 0.0) for c in range(2)], axis=0)
            a0 = jnp.where(first > 0.5, a, 0.0)
            av[0, :, cols] = a0.astype(BF16)
            av[1, :, cols] = (a - a0).astype(BF16)
            return carry

        lax.fori_loop(0, ff // NT, up2, 0)

        @pl.when(s >= RING)
        def _():
            wait_first(s - RING)

        def down(n, carry):
            cols = pl.ds(pl.multiple_of(n * WT, WT), WT)
            r = sum(jnp.dot(av[e], w2v[e, :, cols], preferred_element_type=F32) for e in range(2))
            ob[so, :, :, cols] = r.astype(BF16).reshape(2, cap, WT)
            return carry

        lax.fori_loop(0, d_model // WT, down, 0)

        @pl.when(s >= LAG_F)
        def _():
            forward(s - LAG_F)

        start_first(s)
        chain.serve(s + 3)
        late = s - LAG_C
        odd = lax.rem(late + 2 * steps, 2)

        @pl.when(jnp.logical_and(late >= 0, odd == 0))
        def _():
            fetch(lax.div(late, 2))

        @pl.when(jnp.logical_and(late >= 0, odd == 1))
        def _():
            combine(lax.div(late, 2))

        @pl.when(s + 1 < steps)
        def _():
            arrive(s + 1)

        return carry

    lax.fori_loop(0, steps, step, 0)
    for s in range(steps - LAG_F, steps):
        forward(s)
    for n in range(steps + 3, chain.turns):
        chain.serve(n)
    chain.finish()


    is_h = jnp.logical_and(at.x == lax.rem(at.y, 2), at.c == lax.div(at.y, 2))
    hs = lax.div(at.y + side - 1, side) * loc
    for i, (w, h, v) in enumerate(((w1, h1, w1v), (w3, h3, w3v), (w2, h2, w2v))):

        @pl.when(is_h)
        def _():
            pltpu.make_async_copy(w.at[hs], v.at[0], w_sem.at[i]).start()

        @pl.when(jnp.logical_not(is_h))
        def _():
            pltpu.make_async_copy(h, v.at[0], w_sem.at[i]).start()

    rows0.start()
    begun = (steps - LAG_C) // 2
    if (steps - LAG_C) % 2:
        raise ValueError("odd lag")

    def drain(p, carry):
        fetch(p)
        combine(p)
        return carry

    lax.fori_loop(begun, HOT_AT, drain, 0)
    fetch(HOT_AT)
    for i, (h, v) in enumerate(((h1, w1v), (h3, w3v), (h2, w2v))):
        pltpu.make_async_copy(h, v.at[0], w_sem.at[i]).wait()
    rows0.wait()
    for i in range(td // m2):
        part = slice(i * m2, (i + 1) * m2)

        def up1(f, carry):
            cols = pl.ds(pl.multiple_of(f * NT, NT), NT)
            u = jnp.dot(xs[part, :], w1v[0, :, cols], preferred_element_type=F32)
            v = jnp.dot(xs[part, :], w3v[0, :, cols], preferred_element_type=F32)
            av[0, :, cols] = (jax.nn.silu(u) * v).astype(BF16)
            return carry

        lax.fori_loop(0, ff // NT, up1, 0)

        def down1(n, carry):
            cols = pl.ds(pl.multiple_of(n * WT, WT), WT)
            r = jnp.dot(av[0], w2v[0, :, cols], preferred_element_type=F32).astype(BF16).astype(F32)
            g = gh[part, :]
            yacc[part, cols] += jnp.where(g > 0.0, g * r, 0.0)
            return carry

        lax.fori_loop(0, d_model // WT, down1, 0)

    combine(HOT_AT)
    lax.fori_loop(HOT_AT + 1, steps // 2, drain, 0)

    def out(n, carry):
        cols = pl.ds(pl.multiple_of(n * NT, NT), NT)
        xs[:, cols] = yacc[:, cols].astype(BF16)
        return carry

    lax.fori_loop(0, d_model // NT, out, 0)
    done = pltpu.make_async_copy(xs, y, xk.at[0])
    done.start()


    for cp in sends + fwd[0] + fwd[1]:
        cp.wait_send()
    for d in range(side):
        for c in range(2):
            if d:
                count_send(d, c).wait_send()
    count_send(0, 1 - at.c).wait_send()

    def sent(j, carry):
        k, d, c = lax.div(j, 2 * side), lax.rem(lax.div(j, 2), side), lax.rem(j, 2)
        for t in sides:

            @pl.when(jnp.logical_or(d != 0, c != at.c))
            def _():
                remote(t["sb"].at[k, d, c], t["rv"].at[k, d, c], t["ss"].at[k, d, c], t["rs"].at[k, d, c], along(0, 1, at.c)).wait_send()

        return carry

    lax.fori_loop(0, 2 * side * side, sent, 0)

    def sent1(s, carry):
        wait_first(s)
        return carry

    lax.fori_loop(steps - RING, steps, sent1, 0)

    def sent2(s, carry):
        @pl.when(kind(s)[0])
        def _():
            for h in range(2):
                for cp in second_hop(s, h)[1]:
                    cp.wait_send()

        return carry

    lax.fori_loop(0, steps, sent2, 0)
    done.wait()


def plan(ridx, gates, p, experts):
    td, k = ridx.shape
    ids = jnp.arange(experts, dtype=ridx.dtype)
    hit = ridx[:, :, None] == ids
    g = jnp.sum(jnp.where(hit, gates.astype(F32)[:, :, None], 0.0), axis=1)
    m = jnp.logical_and(jnp.any(hit, axis=1), ids[None, :] > 0)
    mb = m.astype(BF16)
    tri = (jnp.arange(td)[:, None] > jnp.arange(td)[None, :]).astype(BF16)
    rank = jnp.dot(tri, mb, preferred_element_type=F32)
    cnt = jnp.sum(m.astype(F32), axis=0)
    loc = experts // p
    before = jnp.cumsum(cnt.reshape(p, loc), axis=1) - cnt.reshape(p, loc)
    pos = jnp.where(m, rank + before.reshape(-1), -1.0)
    return pos.T, g.T


def solution(mesh):
    p = mesh.shape["ep"]
    side = math.isqrt(p // 2)
    want = [(y * side + y % 2) * 2 + y // 2 for y in range(side)]
    if side != 4 or sorted(holder_list(p)) != sorted(want) or holder_list(p)[0] != want[0]:
        raise ValueError("unknown placement")

    def local(x, ridx, gates, w1, w3, w2):
        td, d = x.shape
        k = ridx.shape[1]
        slots, _, ff = w1.shape
        loc = slots - 1
        cap = td * k // p
        cl = d // 4
        cr = d - cl
        steps = side * side
        pt, gt = plan(ridx, gates, p, p * loc)
        pc = pt.reshape(side, side, 2 * loc, td)
        ml, mr = pc, pc.transpose(1, 0, 2, 3)

        def hbm(*shape):
            return jax.ShapeDtypeStruct(shape, BF16)

        dma = pltpu.SemaphoreType.DMA
        y = pl.pallas_call(
            functools.partial(layer_kernel, side, cap, loc),
            out_shape=[hbm(td, d), hbm(side, td, cl), hbm(side, td, cr)]
            + [hbm(side, side, 2, cap, c) for c in (cl, cr)] * 2
            + [hbm(*w.shape[1:]) for w in (w1, w3, w2)]
            + [hbm(steps, 2, cap, d // 2)] * 4,
            in_specs=[ANY] * 6 + [VMEM] * 3,
            out_specs=[ANY] * 14,
            scratch_shapes=[
                pltpu.VMEM((side, side, 2 * loc, td), F32),
                pltpu.VMEM((side, side, 2 * loc, td), F32),
                pltpu.VMEM((2 * cap, td), BF16),
                pltpu.VMEM((side, 2, side, 8, 128), F32),
                pltpu.VMEM((side, 2, side, 8, 128), F32),
                pltpu.VMEM((2, d, ff), BF16),
                pltpu.VMEM((2, d, ff), BF16),
                pltpu.VMEM((2, ff, d), BF16),
                pltpu.VMEM((2, 2, cap, cl), BF16),
                pltpu.VMEM((2, 2, cap, cr), BF16),
                pltpu.VMEM((td, d), BF16),
                pltpu.VMEM((2, 2 * cap, ff), BF16),
                pltpu.VMEM((RING, 2, cap, d), BF16),
                pltpu.VMEM((2, 2, cap, d // 2), BF16),
                pltpu.VMEM((2, 2, cap, d // 2), BF16),
                pltpu.VMEM((4 * cap, td), BF16),
                pltpu.VMEM((td, d), F32),
            ]
            + [dma((2, side))] * 4
            + [dma((2,)), dma((2, side)), dma((2,)), dma((side, 2)), dma((side, 2))]
            + [dma((side, side, 2))] * 4
            + [dma((3,)), dma((2, 4)), dma((2, 2)), dma((2,))]
            + [dma((steps, 2))] * 8
            + [dma((12 * PARTS,))] * 4,
            compiler_params=pltpu.CompilerParams(collective_id=0, has_side_effects=True, vmem_limit_bytes=67043328),
            name="layer",
        )(x, ml, mr, w1, w3, w2, pc.reshape(steps, 2 * loc, td), gt.reshape(steps, 2 * loc, td), gt[0].reshape(td, 1))[0]
        return y

    spec_t = P(("dp", "ep"), None)
    spec_w = P("ep", None, None)
    return jax.shard_map(local, mesh=mesh, in_specs=(spec_t, spec_t, spec_t, spec_w, spec_w, spec_w), out_specs=spec_t, check_vma=False)
```

time: 582 us -> 560 us (0.962)
  starting transfers between devices: 8.31 us -> 0 us
  Pallas kernels: 557 us -> 549 us
    all_to_all x1 -> x0, starting transfers between devices: 8.31 us -> none  [local(): n0 = lax.all_to_all(n0.reshape(p, 1), 'ep', 0, 0, tiled=True).reshape(p)]
    pallas_call x2 -> x1, Pallas kernels: 557 us -> 549 us  [local(): pl.pallas_call(functools.partial(layer_kernel, side, cap, loc), out_shape...]
  transfers between devices with their start and end apart: 1 -> 0, of which waited for: 0 -> 0; matrix products, arithmetic and copies ran while one was open for 1% -> 0% of each run, Pallas kernels for 43% -> 0%
where the time goes in v4:
time: 560 us; the launch traced here: 559 us
  Pallas kernels  549 us (98%)
  local copies, waits for them, and re-layouts  7.41 us (1%)
    pallas_call x1, Pallas kernels, local(): pl.pallas_call(functools.partial(layer_kernel, side, cap, loc), out_shape...  549 us

profile of v4, /device:TPU:99, one launch (start us, length us, event | category | flops | bytes accessed | tf_op | source)
XLA Modules:
  0.0 559.4 jit_solution(4256735841153483767)
XLA Ops:
  0.0 0.7 convert_element_type.9
  0.7 0.9 fusion.1
  1.7 0.2 convert_reduce_fusion
  1.8 0.1 reshape.24
  2.0 0.2 reduce_window_sum.13
  2.1 0.1 reduce_window_sum.14
  2.2 0.4 fusion.3
  2.7 0.9 select_reduce_fusion
  3.6 0.7 reshape.26.gt
  4.4 0.1 reshape.25.ml
  4.4 0.0 copy-start
  4.4 0.8 reshape_reshape.3.pt
  5.2 0.0 copy-done
  5.2 0.7 copy.17
  5.9 0.9 copy.15.gh
  6.9 548.5 %layer.1 = (bf16[768,2048]{1,0:T(8,128)(2,1)}, bf16[4,768,512]{2,1,0:T(8,128)(2,1)}, bf16[4,768,1536]{2,1,0:T(8,128)(2,1)}, bf16[4,4,2,192,512]{4,3,2,1,0:T(8,12...) custom-call(bf16[768,2048]{1,0:T(8,128)(2,1)} %x.1, ...), custom_call_target="tpu_custom_call" | custom-call | tf_op jit(solution)/shard_map/layer/pallas_call | solution.py:703
  555.4 4.0 copy.19
  (3 shorter events, 0.0 us)
Async XLA Ops:
  4.4 0.8 copy-start

commit v5 on v4

--- a/solution.py
+++ b/solution.py
@@ -17,11 +17,12 @@
 CT = 512
 WT = 512
 RING = 6
-LAG_F = 3
+LAG_F = 4
 HOT_AT = 5
 LAG_C = 10
-ORDER = ((0, 0), (0, 1), (0, 3), (1, 1), (2, 0), (0, 2), (2, 1), (3, 1), (1, 3), (2, 3), (3, 0), (1, 2), (1, 0), (3, 2), (2, 2), (3, 3))
-WAIT = 2
+ORDER = ((0, 0), (1, 0), (3, 0), (0, 1), (0, 3), (3, 3), (2, 3), (1, 3), (1, 1), (3, 2), (1, 2), (2, 0), (0, 2), (2, 1), (2, 2), (3, 1))
+EARLY = 3
+WAIT = 14
 PARTS = 4
 
 
@@ -488,6 +489,16 @@
         cp.wait()
     arrive(0)
 
+    def turns(lo, hi):
+        def one(n, carry):
+            chain.serve(n)
+            return carry
+
+        if hi > lo:
+            lax.fori_loop(lo, hi, one, 0)
+
+    turns(3, 3 + EARLY)
+
     def step(s, carry):
         slot, so = lax.rem(s, 2), lax.rem(s, RING)
         for cp in load_x(s):
@@ -513,6 +524,7 @@
             a0 = jnp.where(first > 0.5, a, 0.0)
             av[0, :, cols] = a0.astype(BF16)
             av[1, :, cols] = (a - a0).astype(BF16)
+            chain.serve(s * (ff // NT) + f + 3 + EARLY)
             return carry
 
         lax.fori_loop(0, ff // NT, up2, 0)
@@ -534,7 +546,6 @@
             forward(s - LAG_F)
 
         start_first(s)
-        chain.serve(s + 3)
         late = s - LAG_C
         odd = lax.rem(late + 2 * steps, 2)
 
@@ -555,8 +566,7 @@
     lax.fori_loop(0, steps, step, 0)
     for s in range(steps - LAG_F, steps):
         forward(s)
-    for n in range(steps + 3, chain.turns):
-        chain.serve(n)
+    turns(steps * (ff // NT) + 3 + EARLY, chain.turns)
     chain.finish()
 
 

time: 560 us -> 544 us (0.971); the launches traced: 559 us -> 536 us
  Pallas kernels: 549 us -> 526 us
    pallas_call x1, Pallas kernels: 549 us -> 526 us  [local(): pl.pallas_call(functools.partial(layer_kernel, side, cap, loc), out_shape...]
where the time goes in v5:
time: 544 us; the launch traced here: 536 us
  Pallas kernels  526 us (97%)
  local copies, waits for them, and re-layouts  7.41 us (1%)
    pallas_call x1, Pallas kernels, local(): pl.pallas_call(functools.partial(layer_kernel, side, cap, loc), out_shape...  526 us

profile of v5, /device:TPU:99, one launch (start us, length us, event | category | flops | bytes accessed | tf_op | source)
XLA Modules:
  0.0 536.4 jit_solution(9156432508321718990)
XLA Ops:
  0.0 0.7 convert_element_type.9
  0.7 0.9 fusion.1
  1.7 0.2 convert_reduce_fusion
  1.8 0.1 reshape.24
  2.0 0.2 reduce_window_sum.13
  2.1 0.1 reduce_window_sum.14
  2.2 0.4 fusion.3
  2.7 0.9 select_reduce_fusion
  3.6 0.7 reshape.26.gt
  4.4 0.1 reshape.25.ml
  4.4 0.0 copy-start
  4.4 0.8 reshape_reshape.3.pt
  5.2 0.0 copy-done
  5.2 0.7 copy.17
  5.9 0.9 copy.15.gh
  6.9 525.6 %layer.1 = (bf16[768,2048]{1,0:T(8,128)(2,1)}, bf16[4,768,512]{2,1,0:T(8,128)(2,1)}, bf16[4,768,1536]{2,1,0:T(8,128)(2,1)}, bf16[4,4,2,192,512]{4,3,2,1,0:T(8,12...) custom-call(bf16[768,2048]{1,0:T(8,128)(2,1)} %x.1, ...), custom_call_target="tpu_custom_call" | custom-call | tf_op jit(solution)/shard_map/layer/pallas_call | solution.py:713
  532.5 4.0 copy.19
  (3 shorter events, 0.0 us)
Async XLA Ops:
  4.4 0.8 copy-start

commit v6 on v5

--- a/solution.py
+++ b/solution.py
@@ -16,12 +16,13 @@
 NT = 256
 CT = 512
 WT = 512
+CUT = 4
 RING = 6
 LAG_F = 4
 HOT_AT = 5
 LAG_C = 10
 ORDER = ((0, 0), (1, 0), (3, 0), (0, 1), (0, 3), (3, 3), (2, 3), (1, 3), (1, 1), (3, 2), (1, 2), (2, 0), (0, 2), (2, 1), (2, 2), (3, 1))
-EARLY = 3
+EARLY = 5
 WAIT = 14
 PARTS = 4
 
@@ -55,6 +56,10 @@
         for d in near:
             pl.semaphore_signal(bar, inc=1, device_id=d, device_id_type=MESH)
         pl.semaphore_wait(bar, len(near))
+
+
+def tiles(width, most):
+    return [(lo, min(most, width - lo)) for lo in range(0, width, most)]
 
 
 def remote(src, dst, ssem, rsem, dev):
@@ -161,9 +166,9 @@
 
 
 def layer_kernel(
-    side, cap, loc, x, ml, mr, w1, w3, w2, pt, gt, gh,
+    side, cap, loc, x, w1, w3, w2, ridx, gates,
     y, xlh, xrh, sbl, sbr, recvl, recvr, h1, h3, h2, rell, relr, retl, retr,
-    mlv, mrv, sel, cntb, nrec, w1v, w3v, w2v, xbl, xbr, xs, av, ob, ocl, ocr, gm, yacc,
+    pt, gt, mlv, mrv, sel, cntb, nrec, w1v, w3v, w2v, xbl, xbr, xs, av, ob, ocl, ocr, gm, yacc, gh,
     m_s, m_r, ag_s, ag_r, xk, st, own, n_s, n_r, s_l, r_l, s_r, r_r,
     w_sem, x_sem, c_sem, k_sem, s1l, s1r, r1l, r1r, s2l, s2r, r2l, r2r, *w_sems,
 ):
@@ -177,30 +182,57 @@
     m2 = 2 * cap
     half, last = td // 2, side - 1
     lside, rside = sides = (
-        dict(i=0, axis=0, lo=0, width=cl, xh=xlh, m=ml, mv=mlv, sb=sbl, rv=recvl, ss=s_l, rs=r_l),
-        dict(i=1, axis=1, lo=cl, width=cr, xh=xrh, m=mr, mv=mrv, sb=sbr, rv=recvr, ss=s_r, rs=r_r),
+        dict(i=0, axis=0, lo=0, width=cl, xh=xlh, m=lambda n: pt.at[n], mv=mlv, sb=sbl, rv=recvl, ss=s_l, rs=r_l),
+        dict(i=1, axis=1, lo=cl, width=cr, xh=xrh, m=lambda n: pt.at[:, n], mv=mrv, sb=sbr, rv=recvr, ss=s_r, rs=r_r),
     )
 
     def along(a, k, c):
         return at.dev(k, 0, c) if a == 0 else at.dev(0, k, c)
 
 
-    mine = [pltpu.make_async_copy(t["m"].at[at.y if t["axis"] == 0 else at.x], t["mv"].at[0], own.at[t["i"]]) for t in sides]
-    for cp in mine:
-        cp.start()
     rows0 = pltpu.make_async_copy(x, xs, xk.at[0])
     rows0.start()
     at.greet()
     sends = []
     for t in sides:
-        i, a, here = t["i"], t["axis"], at.y if t["axis"] == 0 else at.x
-        for k in range(1, side):
-            sends.append(remote(t["m"].at[lax.rem(here + k, side)], t["mv"].at[side - k], m_s.at[i, k], m_r.at[i, side - k], along(a, k, at.c)))
+        i, a = t["i"], t["axis"]
         src = x.at[:, pl.ds(t["lo"], t["width"])]
         sends.append(remote(src, t["xh"].at[last], ag_s.at[i, 0], ag_r.at[i, last], along(a, 1, at.c)))
         sends.append(remote(src, t["xh"].at[1], ag_s.at[i, 1], ag_r.at[i, 1], along(a, last, at.c)))
     for cp in sends:
         cp.start()
+
+
+    rows = 2 * loc
+    e = lax.broadcasted_iota(jnp.int32, (rows * steps, td), 0)
+    gates = gates[...].astype(F32)
+    m = jnp.zeros((rows * steps, td), F32)
+    g = jnp.zeros((rows * steps, td), F32)
+    for n in range(ridx.shape[0]):
+        hit = ridx[n : n + 1, :] == e
+        m = m + jnp.where(hit, 1.0, 0.0)
+        g = g + jnp.where(hit, gates[n : n + 1, :], 0.0)
+    m = jnp.where(e > 0, m, 0.0)
+    earlier = lax.broadcasted_iota(jnp.int32, (td, td), 0) < lax.broadcasted_iota(jnp.int32, (td, td), 1)
+    rank = jnp.dot(m.astype(BF16), jnp.where(earlier, 1.0, 0.0).astype(BF16), preferred_element_type=F32)
+    cnt = jnp.broadcast_to(jnp.sum(m, axis=1, keepdims=True), (rows * steps, 128))
+    before = jnp.where(lax.rem(e[:, 0:128], loc) > 0, pltpu.roll(cnt, 1, 0), 0.0)
+    pos = jnp.where(m > 0.0, rank + before[:, 0:1], -1.0)
+    for n in range(steps):
+        pt[n // side, n % side] = pos[n * rows : (n + 1) * rows, :]
+        gt[n // side, n % side] = g[n * rows : (n + 1) * rows, :]
+    mlv[0] = pt[at.y]
+    for n in range(side):
+        mrv[0, n] = pt[n, at.x]
+    gh[...] = jnp.transpose(jnp.broadcast_to(gt[0, 0, 0:1, :], (128, td)))
+    metas = []
+    for t in sides:
+        i, a, here = t["i"], t["axis"], at.y if t["axis"] == 0 else at.x
+        for k in range(1, side):
+            metas.append(remote(t["m"](lax.rem(here + k, side)), t["mv"].at[side - k], m_s.at[i, k], m_r.at[i, side - k], along(a, k, at.c)))
+    for cp in metas:
+        cp.start()
+    sends += metas
     weights = [pltpu.make_async_copy(w.at[pl.ds(0, 2)], v, w_sem.at[i]) for i, (w, v) in enumerate(((w1, w1v), (w3, w3v), (w2, w2v)))]
     for cp in weights:
         cp.start()
@@ -225,13 +257,10 @@
                     hit = jnp.logical_or(r == p0, r == p1)
                     sel[c * cap : (c + 1) * cap, :] = jnp.where(hit, 1.0, 0.0).astype(BF16)
 
-                def col(n, carry):
-                    cols = pl.ds(pl.multiple_of(t["lo"] + n * WT, WT), WT)
+                for lo, n in tiles(t["width"], WT):
+                    cols = pl.ds(t["lo"] + lo, n)
                     o = jnp.dot(sel[...], xs[:, cols], preferred_element_type=F32).astype(BF16)
-                    ob[d, :, :, cols] = o.reshape(2, cap, WT)
-                    return carry
-
-                lax.fori_loop(0, t["width"] // WT, col, 0)
+                    ob[d, :, :, cols] = o.reshape(2, cap, n)
             for t in sides:
                 both, other, self_ = staged(t, k, d)
 
@@ -292,8 +321,6 @@
     def count_send(d, c):
         return remote(cntb.at[d, c], nrec.at[(side - d) % side, at.c], n_s.at[d, c], n_r.at[(side - d) % side, at.c], along(1, d, c))
 
-    for cp in mine:
-        cp.wait()
     rows0.wait()
     pack(0)
     yacc[...] = jnp.zeros_like(yacc)
@@ -368,6 +395,7 @@
             cp.start()
 
     outs = (pl.ds(0, co), pl.ds(co, co))
+    done = [pltpu.make_async_copy(xs.at[:, cols], y.at[:, cols], xk.at[h]) for h, cols in enumerate(outs)]
     halves = ((rell, retl, s1l, r1l, s2l, r2l), (relr, retr, s1r, r1r, s2r, r2r))
 
     def first_hop(s, h):
@@ -453,18 +481,18 @@
 
                 pltpu.make_async_copy(ret.at[s], oc.at[i], c_sem.at[h, i]).start()
 
-    def combine(p):
+    def combine(p, end=False):
         for i in range(2):
             dy, dx = where_to(2 * p + i)
             oy = at.c * dy + (1 - at.c) * (side - dy)
             ox = at.c * dx + (1 - at.c) * (side - dx)
-            chip = lax.rem(at.y + oy, side) * side + lax.rem(at.x + ox, side)
+            cy, cx = lax.rem(at.y + oy, side), lax.rem(at.x + ox, side)
             r = lax.broadcasted_iota(jnp.int32, (cap, td), 0).astype(F32)
             for c in range(2):
                 g = jnp.zeros((cap, td), F32)
                 for j in range(2):
                     row = 2 * c + j
-                    g = g + jnp.where(r == pt[chip, row : row + 1, :], gt[chip, row : row + 1, :], 0.0)
+                    g = g + jnp.where(r == pt[cy, cx, row : row + 1, :], gt[cy, cx, row : row + 1, :], 0.0)
                 lo = (2 * i + c) * cap
                 gm[lo : lo + cap, :] = g.astype(BF16)
         for h, oc in enumerate((ocl, ocr)):
@@ -475,10 +503,16 @@
                 cols = pl.ds(pl.multiple_of(n * CT, CT), CT)
                 to = pl.ds(pl.multiple_of(h * co + n * CT, CT), CT)
                 b = oc[:, :, :, cols].reshape(2 * m2, CT)
-                yacc[:, to] += lax.dot_general(gm[...], b, (((0,), (0,)), ((), ())), preferred_element_type=F32)
+                new = yacc[:, to] + lax.dot_general(gm[...], b, (((0,), (0,)), ((), ())), preferred_element_type=F32)
+                if end:
+                    xs[:, to] = new.astype(BF16)
+                else:
+                    yacc[:, to] = new
                 return carry
 
             lax.fori_loop(0, co // CT, col, 0)
+            if end:
+                done[h].start()
 
     for d in range(side):
         for c in range(2):
@@ -506,11 +540,11 @@
         cuts = [jnp.max(nrec[dx, j, dy]) for j, (dy, dx) in enumerate(ends(s))]
         for c in range(2):
             for xb, lo, width in ((xbl, 0, cl), (xbr, cl, cr)):
-                for n in range(width // NT):
-                    v = xb[slot, c, :, n * NT : (n + 1) * NT].astype(F32)
-                    first = lax.broadcasted_iota(jnp.int32, (cap, NT), 0).astype(F32) < cuts[c]
+                for n, wide in tiles(width, NT):
+                    v = xb[slot, c, :, n : n + wide].astype(F32)
+                    first = lax.broadcasted_iota(jnp.int32, (cap, wide), 0).astype(F32) < cuts[c]
                     z = jnp.zeros_like(v)
-                    to = slice(lo + n * NT, lo + (n + 1) * NT)
+                    to = slice(lo + n, lo + n + wide)
                     xs[c * cap : (c + 1) * cap, to] = jnp.where(first, v, z).astype(BF16)
                     xs[m2 + c * cap : m2 + (c + 1) * cap, to] = jnp.where(first, z, v).astype(BF16)
 
@@ -612,23 +646,16 @@
         def down1(n, carry):
             cols = pl.ds(pl.multiple_of(n * WT, WT), WT)
             r = jnp.dot(av[0], w2v[0, :, cols], preferred_element_type=F32).astype(BF16).astype(F32)
-            g = gh[part, :]
+            g = gh[part, 0:1]
             yacc[part, cols] += jnp.where(g > 0.0, g * r, 0.0)
             return carry
 
         lax.fori_loop(0, d_model // WT, down1, 0)
 
     combine(HOT_AT)
-    lax.fori_loop(HOT_AT + 1, steps // 2, drain, 0)
-
-    def out(n, carry):
-        cols = pl.ds(pl.multiple_of(n * NT, NT), NT)
-        xs[:, cols] = yacc[:, cols].astype(BF16)
-        return carry
-
-    lax.fori_loop(0, d_model // NT, out, 0)
-    done = pltpu.make_async_copy(xs, y, xk.at[0])
-    done.start()
+    lax.fori_loop(HOT_AT + 1, steps // 2 - 1, drain, 0)
+    fetch(steps // 2 - 1)
+    combine(steps // 2 - 1, end=True)
 
 
     for cp in sends + fwd[0] + fwd[1]:
@@ -667,23 +694,8 @@
         return carry
 
     lax.fori_loop(0, steps, sent2, 0)
-    done.wait()
-
-
-def plan(ridx, gates, p, experts):
-    td, k = ridx.shape
-    ids = jnp.arange(experts, dtype=ridx.dtype)
-    hit = ridx[:, :, None] == ids
-    g = jnp.sum(jnp.where(hit, gates.astype(F32)[:, :, None], 0.0), axis=1)
-    m = jnp.logical_and(jnp.any(hit, axis=1), ids[None, :] > 0)
-    mb = m.astype(BF16)
-    tri = (jnp.arange(td)[:, None] > jnp.arange(td)[None, :]).astype(BF16)
-    rank = jnp.dot(tri, mb, preferred_element_type=F32)
-    cnt = jnp.sum(m.astype(F32), axis=0)
-    loc = experts // p
-    before = jnp.cumsum(cnt.reshape(p, loc), axis=1) - cnt.reshape(p, loc)
-    pos = jnp.where(m, rank + before.reshape(-1), -1.0)
-    return pos.T, g.T
+    for cp in done:
+        cp.wait()
 
 
 def solution(mesh):
@@ -699,12 +711,11 @@
         slots, _, ff = w1.shape
         loc = slots - 1
         cap = td * k // p
-        cl = d // 4
+        cl = CUT * d // 16
         cr = d - cl
         steps = side * side
-        pt, gt = plan(ridx, gates, p, p * loc)
-        pc = pt.reshape(side, side, 2 * loc, td)
-        ml, mr = pc, pc.transpose(1, 0, 2, 3)
+        if loc != 2:
+            raise ValueError("unknown placement")
 
         def hbm(*shape):
             return jax.ShapeDtypeStruct(shape, BF16)
@@ -716,9 +727,11 @@
             + [hbm(side, side, 2, cap, c) for c in (cl, cr)] * 2
             + [hbm(*w.shape[1:]) for w in (w1, w3, w2)]
             + [hbm(steps, 2, cap, d // 2)] * 4,
-            in_specs=[ANY] * 6 + [VMEM] * 3,
+            in_specs=[ANY] * 4 + [VMEM] * 2,
             out_specs=[ANY] * 14,
             scratch_shapes=[
+                pltpu.VMEM((side, side, 2 * loc, td), F32),
+                pltpu.VMEM((side, side, 2 * loc, td), F32),
                 pltpu.VMEM((side, side, 2 * loc, td), F32),
                 pltpu.VMEM((side, side, 2 * loc, td), F32),
                 pltpu.VMEM((2 * cap, td), BF16),
@@ -736,6 +749,7 @@
                 pltpu.VMEM((2, 2, cap, d // 2), BF16),
                 pltpu.VMEM((4 * cap, td), BF16),
                 pltpu.VMEM((td, d), F32),
+                pltpu.VMEM((td, 128), F32),
             ]
             + [dma((2, side))] * 4
             + [dma((2,)), dma((2, side)), dma((2,)), dma((side, 2)), dma((side, 2))]
@@ -745,7 +759,7 @@
             + [dma((12 * PARTS,))] * 4,
             compiler_params=pltpu.CompilerParams(collective_id=0, has_side_effects=True, vmem_limit_bytes=67043328),
             name="layer",
-        )(x, ml, mr, w1, w3, w2, pc.reshape(steps, 2 * loc, td), gt.reshape(steps, 2 * loc, td), gt[0].reshape(td, 1))[0]
+        )(x, w1, w3, w2, ridx.T, gates.T)[0]
         return y
 
     spec_t = P(("dp", "ep"), None)

time: 544 us -> 530 us (0.974)
  no operation moved by 1% of the time
where the time goes in v6:
time: 530 us; the launch traced here: 527 us
  Pallas kernels  523 us (99%)
    pallas_call x1, Pallas kernels, local(): pl.pallas_call(functools.partial(layer_kernel, side, cap, loc), out_shape...  523 us

profile of v6, /device:TPU:99, one launch (start us, length us, event | category | flops | bytes accessed | tf_op | source)
XLA Modules:
  0.0 526.6 jit_solution(9187397047373793621)
XLA Ops:
  0.0 522.6 %layer.1 = (bf16[768,2048]{1,0:T(8,128)(2,1)}, bf16[4,768,512]{2,1,0:T(8,128)(2,1)}, bf16[4,768,1536]{2,1,0:T(8,128)(2,1)}, bf16[4,4,2,192,512]{4,3,2,1,0:T(8,12...) custom-call(bf16[768,2048]{1,0:T(8,128)(2,1)} %x.1, ...), custom_call_target="tpu_custom_call" | custom-call | tf_op jit(solution)/shard_map/layer/pallas_call | solution.py:724
  522.6 4.0 copy.8

commit v7 on v6

--- a/solution.py
+++ b/solution.py
@@ -22,7 +22,7 @@
 HOT_AT = 5
 LAG_C = 10
 ORDER = ((0, 0), (1, 0), (3, 0), (0, 1), (0, 3), (3, 3), (2, 3), (1, 3), (1, 1), (3, 2), (1, 2), (2, 0), (0, 2), (2, 1), (2, 2), (3, 1))
-EARLY = 5
+EARLY = 7
 WAIT = 14
 PARTS = 4
 

time: 530 us -> 537 us (1.013); the launches traced: 527 us -> 526 us
  no operation moved by 1% of the time
where the time goes in v7:
time: 537 us; the launch traced here: 526 us
  Pallas kernels  522 us (97%)
    pallas_call x1, Pallas kernels, local(): pl.pallas_call(functools.partial(layer_kernel, side, cap, loc), out_shape...  522 us

profile of v7, /device:TPU:99, one launch (start us, length us, event | category | flops | bytes accessed | tf_op | source)
XLA Modules:
  0.0 526.1 jit_solution(5228681889116259453)
XLA Ops:
  0.0 522.1 %layer.1 = (bf16[768,2048]{1,0:T(8,128)(2,1)}, bf16[4,768,512]{2,1,0:T(8,128)(2,1)}, bf16[4,768,1536]{2,1,0:T(8,128)(2,1)}, bf16[4,4,2,192,512]{4,3,2,1,0:T(8,12...) custom-call(bf16[768,2048]{1,0:T(8,128)(2,1)} %x.1, ...), custom_call_target="tpu_custom_call" | custom-call | tf_op jit(solution)/shard_map/layer/pallas_call | solution.py:724
  522.1 4.0 copy.8
